TPU v7x, 512 devices: a whole 4x8x8 slice. The times are simulated.
512 devices in a mesh: seq: 32 (over x, y_hi, core), tp: 16 (over z, y_lo).
Axes of the slice: x: 4, y: 8 (y_hi: 4, y_lo: 2; y = y_hi * 2 + y_lo), z: 8, core: 2. Of those that a mesh axis runs over, the one named last changes fastest.
Arguments:
- hidden: bfloat16 [16384, 4096], P('seq', 'tp'), may hold values from -6 to 6
- norm_gain: float32 [4096], P('tp'), may hold values from 0.5 to 1.5
- rank_down: bfloat16 [4096, 1024], P('tp'), may hold values from -0.09375 to 0.09375
- gate_up: bfloat16 [1024, 4096], P(None, 'tp'), may hold values from -0.1875 to 0.1875
- value_up: bfloat16 [1024, 4096], P(None, 'tp'), may hold values from -0.1875 to 0.1875
- state_up: bfloat16 [1024, 1024], P(None, 'tp'), may hold values from -0.1875 to 0.1875
- step_up: bfloat16 [1024, 64], P(None, 'tp'), may hold values from -0.1875 to 0.1875
- conv_value: float32 [4, 4096], P(None, 'tp'), may hold values from -3 to 3
- conv_state: float32 [4, 1024], P(None, 'tp'), may hold values from -3 to 3
- step_bias: float32 [64], P('tp'), may hold values from -6.9 to -2.3
- decay_log: float32 [64], P('tp'), may hold values from -11 to 2.77
- skip_gain: float32 [64], P('tp'), may hold values from 0.5 to 1.5
- gate_gain: float32 [4096], P('tp'), may hold values from 0.5 to 1.5
- out_down: bfloat16 [4096, 1024], P('tp'), may hold values from -0.09375 to 0.09375
- out_up: bfloat16 [1024, 4096], P(None, 'tp'), may hold values from -0.1875 to 0.1875
Outputs:
- block_out: bfloat16 [16384, 4096], P('seq', 'tp')
All inputs are finite; a program needn't handle non-finite values.
Results may differ from a plain program's by a relative error of at most 0.012.
Values may be sent and summed in bfloat16 or wider, within the bound.
A program may use at most 64 MiB of HBM per device.

v0:
```python
import jax
import jax.numpy as jnp
from jax import lax
from jax.sharding import Mesh
from jax.sharding import PartitionSpec as P

HEAD_DIM = 64
NSTATE = 128
GROUPS = 4
SEQ = ("seq_0", "seq_1", "seq_2")


epsilon = 1e-05
highest = lax.Precision.HIGHEST


def sent_to_all(shard, axis):
    copies = jnp.broadcast_to(shard, (lax.axis_size(axis), *shard.shape))
    return lax.all_to_all(copies, axis, split_axis=0, concat_axis=0, tiled=True)


def over_copies(shard, axis):
    return sent_to_all(shard, axis).sum(axis=0)


def in_blocks(shard, dim, peers):
    before, after = (shard.shape[:dim], shard.shape[dim + 1 :])
    return jnp.moveaxis(shard.reshape(*before, peers, -1, *after), dim, 0)


def sent_and_summed(shard, axis, dim):
    peers = lax.axis_size(axis)
    tiles = lax.all_to_all(in_blocks(shard, dim, peers), axis, 0, 0, tiled=True)
    return jnp.sum(tiles, axis=0)


def laid_out(tiles, dim):
    shape = list(tiles.shape[1:])
    shape[dim] *= tiles.shape[0]
    return jnp.moveaxis(tiles, 0, dim).reshape(shape)


def collect(shard, axis, dim):
    tiles = sent_to_all(shard, axis)
    return laid_out(tiles, dim)


def shifted(shard, axis, by):
    peers = lax.axis_size(axis)
    pairs = [(i, i + by) for i in range(peers) if 0 <= i + by < peers]
    return lax.ppermute(shard, axis, pairs)


def filled_with(shard, identity):
    return jax.tree.map(
        lambda part, zero: jnp.zeros_like(part) + jnp.asarray(zero, part.dtype), shard, identity
    )


def entering(shard, axes, combine, identity):
    before = start = filled_with(shard, identity)
    running = shard
    for axis in reversed(axes):
        peers, place = (lax.axis_size(axis), lax.axis_index(axis))
        pieces = jax.tree.map(lambda part: lax.all_gather(part, axis), running)
        inside, running = (start, start)
        for k in range(peers):
            passed = k < place
            running = combine(running, jax.tree.map(lambda part: part[k], pieces))
            inside = jax.tree.map(lambda new, old: jnp.where(passed, new, old), running, inside)
        before = combine(inside, before)
    return before


def summed_on_arrival(shard, axis, dim):
    tiles = in_blocks(shard, dim, lax.axis_size(axis))
    arrived = lax.all_to_all(tiles, axis, split_axis=0, concat_axis=0, tiled=True)
    return arrived.astype(jnp.float32).sum(axis=0)


def contract_rows(left, right):
    return lax.dot_general(
        left, right, (((0,), (0,)), ((), ())), preferred_element_type=jnp.float32
    )


def contract_columns(columns, rows):
    return lax.dot_general(
        columns, rows, (((0,), (1,)), ((), ())), preferred_element_type=jnp.float32
    )


def depthwise(rim_rows, current, weights):
    joined = jnp.concatenate([rim_rows, current], axis=0).astype(jnp.float32)
    length = current.shape[0]
    result = jnp.zeros(current.shape, jnp.float32)
    for offset in range(weights.shape[0]):
        result = result + weights[offset] * joined[offset : offset + length]
    return jax.nn.silu(result).astype(jnp.bfloat16)


def on_device(
    hidden,
    norm_gain,
    rank_down,
    gate_up,
    value_up,
    state_up,
    step_up,
    conv_value,
    conv_state,
    step_bias,
    decay_log,
    skip_gain,
    gate_gain,
    out_down,
    out_up,
):
    tokens = hidden.shape[0]
    tp_count = lax.axis_size("tp")
    tp_index = lax.axis_index("tp")
    model_width = hidden.shape[1] * tp_count
    hidden_wide = hidden.astype(jnp.float32)
    local_squares = jnp.sum(hidden_wide * hidden_wide, axis=1)
    scaled = (hidden_wide * norm_gain).astype(jnp.bfloat16)
    up_weights = (gate_up, value_up, state_up, step_up)
    total_squares = over_copies(local_squares, "tp")
    factor = lax.rsqrt(total_squares / model_width + epsilon)
    columns = rank_down
    rank_share = sent_and_summed(contract_columns(columns, scaled), "tp", 0)
    reduced_rows = (rank_share * factor[None, :]).astype(jnp.bfloat16)
    row_block = collect(reduced_rows, "tp", 0)
    projected = tuple((contract_rows(row_block, weight) for weight in up_weights))
    gate_pre = projected[0].astype(jnp.bfloat16)
    value_pre = projected[1].astype(jnp.bfloat16)
    state_pre = projected[2].astype(jnp.bfloat16)
    step_pre = projected[3].astype(jnp.bfloat16)
    rim_start = tokens - conv_value.shape[0] + 1
    rim_value, rim_state = shifted((value_pre[rim_start:], state_pre[rim_start:]), SEQ, 1)
    value_act = depthwise(rim_value, value_pre, conv_value)
    state_act = depthwise(rim_state, state_pre, conv_state)
    state_all = collect(state_act, "tp", 1)
    heads_local = decay_log.shape[0]
    heads_total = heads_local * tp_count
    group_index = tp_index * heads_local // (heads_total // GROUPS)
    inward = lax.dynamic_slice_in_dim(state_all, group_index * NSTATE, NSTATE, 1).astype(
        jnp.float32
    )
    outward = lax.dynamic_slice_in_dim(
        state_all, (GROUPS + group_index) * NSTATE, NSTATE, 1
    ).astype(jnp.float32)
    step_size = jax.nn.softplus(step_pre.astype(jnp.float32) + step_bias)
    log_decay = jnp.cumsum(-jnp.exp(decay_log) * step_size, axis=0)
    values = value_act.astype(jnp.float32).reshape(tokens, heads_local, HEAD_DIM)
    coupling = jnp.dot(outward, inward.T, precision=highest)
    positions = jnp.arange(tokens)
    causal = positions[:, None] >= positions[None, :]
    spread = log_decay.T[:, :, None] - log_decay.T[:, None, :]
    attenuation = jnp.where(causal[None], jnp.exp(jnp.where(causal[None], spread, 0.0)), 0.0)
    mixing = coupling[None] * attenuation * step_size.T[:, None, :]
    within = jnp.einsum("hts,shp->thp", mixing, values, precision=highest)
    ending = jnp.exp(log_decay[-1][None, :] - log_decay) * step_size
    local_state = jnp.einsum("sh,shp,sn->hpn", ending, values, inward, precision=highest)
    local_decay = jnp.exp(log_decay[-1])

    def combine(earlier, later):
        return (earlier[0] * later[0], later[0][:, None, None] * earlier[1] + later[1])

    prefix = entering(
        (local_decay, local_state),
        SEQ,
        combine,
        (jnp.ones_like(local_decay), jnp.zeros_like(local_state)),
    )
    incoming = prefix[1]
    carried_in = jnp.exp(log_decay)[:, :, None] * jnp.einsum(
        "tn,hpn->thp", outward, incoming, precision=highest
    )
    mixed = (within + carried_in + skip_gain[None, :, None] * values).reshape(
        tokens, heads_local * HEAD_DIM
    )
    gated = mixed * jax.nn.silu(gate_pre.astype(jnp.float32))
    group_width = heads_total * HEAD_DIM // GROUPS
    selector = (jnp.arange(GROUPS) == group_index).astype(jnp.float32)
    group_sums = over_copies(jnp.sum(gated * gated, axis=1)[:, None] * selector[None, :], "tp")
    own_sum = jnp.sum(group_sums * selector[None, :], axis=1)
    normed = (gated * lax.rsqrt(own_sum / group_width + epsilon)[:, None] * gate_gain).astype(
        jnp.bfloat16
    )
    columns = out_down
    out_share = summed_on_arrival(
        contract_columns(columns, normed).astype(jnp.bfloat16), "tp", 0
    ).astype(jnp.bfloat16)
    update = contract_rows(collect(out_share, "tp", 0), out_up)
    return (hidden_wide + update).astype(jnp.bfloat16)


def solution(mesh):
    finer = Mesh(mesh.devices.reshape(4, 4, 2, mesh.shape["tp"]), ("seq_0", "seq_1", "seq_2", "tp"))
    placed = (
        P(SEQ, "tp"),
        P("tp"),
        P("tp", None),
        P(None, "tp"),
        P(None, "tp"),
        P(None, "tp"),
        P(None, "tp"),
        P(None, "tp"),
        P(None, "tp"),
        P("tp"),
        P("tp"),
        P("tp"),
        P("tp"),
        P("tp", None),
        P(None, "tp"),
    )
    return jax.shard_map(
        on_device, mesh=finer, in_specs=placed, out_specs=P(SEQ, "tp"), check_vma=False
    )
```

profile of v0, /device:TPU:2, one launch (start us, length us, event | category | flops | bytes accessed | tf_op | source)
XLA Modules:
  0.0 269.9 jit_solution(600925571077212565)
XLA Ops:
  0.0 1.2 fusion.25
  1.2 0.6 broadcast_in_dim.34
  1.8 11.4 %all-to-all-start.1 = ((f32[16,1,512]{2,1,0:T(1,128)}), f32[16,1,512]{2,1,0:T(1,128)S(1)}, u32[]{:S(2)}, u32[]{:S(2)}) async-start(f32[16,1,512]{2,1,0:T(1,128)} %broadcast_in_dim.34), calls=%async_computation.1 | async-start | bytes 65536 | tf_op jit(solution)/shard_map/all_to_all | solution.py:19
  13.2 1.4 convolution_bitcast_fusion
  14.6 1.9 copy.42
  16.5 5.3 %all-to-all-done.1 = f32[16,1,512]{2,1,0:T(1,128)S(1)} async-done(((f32[16,1,512]{2,1,0:T(1,128)}), f32[16,1,512]{2,1,0:T(1,128)S(1)}, u32[]{:S(2)}, u32[]{:S(2)}) %all-to-all-start.1) | async-done | bytes 32800 | tf_op jit(solution)/shard_map/all_to_all | solution.py:19
  21.9 3.7 %all-to-all-start = ((f32[16,64,512]{2,1,0:T(8,128)}), f32[16,64,512]{2,1,0:T(8,128)S(1)}, u32[]{:S(2)}, u32[]{:S(2)}) async-start(f32[16,64,512]{2,1,0:T(8,128)} %bitcast.2), calls=%async_computation | async-start | bytes 4194304 | tf_op jit(solution)/shard_map/all_to_all | solution.py:33
  25.6 49.4 %all-to-all-done = f32[16,64,512]{2,1,0:T(8,128)S(1)} async-done(((f32[16,64,512]{2,1,0:T(8,128)}), f32[16,64,512]{2,1,0:T(8,128)S(1)}, u32[]{:S(2)}, u32[]{:S(2)}) %all-to-all-start) | async-done | bytes 2097184 | tf_op jit(solution)/shard_map/all_to_all | solution.py:33
  75.0 0.2 reduce_sum.66
  75.2 0.0 copy-start.11
  75.2 0.0 copy-start.6
  75.2 0.0 copy-start.5
  75.2 0.0 copy-start.3
  75.2 1.1 broadcast_in_dim.62
  76.3 4.1 %all-to-all-start.2 = ((bf16[16,64,512]{2,1,0:T(8,128)(2,1)}), bf16[16,64,512]{2,1,0:T(8,128)(2,1)S(1)}, u32[]{:S(2)}, u32[]{:S(2)}) async-start(bf16[16,64,512]{2,1,0:T(8,128)(2,1)} %broadcast_in_dim.62), calls=%async_computation.2 | async-start | bytes 2097152 | tf_op jit(solution)/shard_map/all_to_all | solution.py:19
  80.5 0.1 iota_compare_fusion
  80.6 26.9 %all-to-all-done.2 = bf16[16,64,512]{2,1,0:T(8,128)(2,1)S(1)} async-done(((bf16[16,64,512]{2,1,0:T(8,128)(2,1)}), bf16[16,64,512]{2,1,0:T(8,128)(2,1)S(1)}, u32[]{:S(2)}, u32[]{:S(2)}) %all-to-all-start.2) | async-done | bytes 1048608 | tf_op jit(solution)/shard_map/all_to_all | solution.py:19
  107.5 0.3 convolution_convert_fusion.3
  107.8 0.1 slice.182
  107.9 1.9 collective-permute-start.1
  109.8 0.5 convolution_convert_fusion.2
  110.3 0.0 copy-start.4
  110.3 0.0 copy-start.8
  110.4 4.6 %collective-permute-start = (bf16[3,256]{1,0:T(4,128)(2,1)S(1)}, bf16[3,256]{1,0:T(4,128)(2,1)S(1)}, u32[]{:S(2)}, u32[]{:S(2)}) collective-permute-start(bf16[3,256]{1,0:T(4,128)(2,1)S(1)} %slice.177), channel_id=1, source_target_pairs={{0,16},{16,32},{32,48},{48,64},{64,80},{80,96},{96,112},{112,128},... | collective-permute-start | bytes 4616 | tf_op jit(solution)/shard_map/ppermute | solution.py:51
  115.0 1.0 collective-permute-done.1
  116.0 0.1 maximum_convert_fusion.1
  116.1 0.2 multiply_convert_fusion.3
  116.3 1.1 broadcast_in_dim.63
  117.4 4.1 %all-to-all-start.3 = ((bf16[16,512,64]{1,2,0:T(8,128)(2,1)}), bf16[16,512,64]{1,2,0:T(8,128)(2,1)S(1)}, u32[]{:S(2)}, u32[]{:S(2)}) async-start(bf16[16,512,64]{1,2,0:T(8,128)(2,1)} %broadcast_in_dim.63), calls=%async_computation.3 | async-start | bytes 2097152 | tf_op jit(solution)/shard_map/all_to_all | solution.py:19
  121.5 0.3 broadcast_multiply_fusion.1
  121.8 1.2 reduce-window.6
  123.0 0.2 slice_reduce_fusion
  123.2 0.2 reduce-window.9
  123.3 0.1 add_bitcast_fusion
  123.4 0.2 exponential_reduce_fusion
  123.6 1.8 all-gather.1
  125.4 16.8 %all-gather.2 = f32[4,1,4]{2,1,0:T(1,128)S(1)} all-gather(f32[1,1,4]{2,1,0:T(1,128)S(1)} %get-tuple-element.33), channel_id=1, replica_groups=mesh['seq_0'=4,'seq_1'=4,'seq_2'=2,'tp'=16] {'seq_1'}, dimensions={0}, use_global_device_ids=true | all-gather | bytes 80 | tf_op jit(solution)/shard_map/all_gather | solution.py:65
  142.2 7.5 %all-gather.3 = f32[4,1,4]{2,1,0:T(1,128)S(1)} all-gather(f32[1,1,4]{2,1,0:T(1,128)S(1)} %get-tuple-element.23), channel_id=1, replica_groups=mesh['seq_0'=4,'seq_1'=4,'seq_2'=2,'tp'=16] {'seq_0'}, dimensions={0}, use_global_device_ids=true | all-gather | bytes 80 | tf_op jit(solution)/shard_map/all_gather | solution.py:65
  149.7 0.1 fusion.106
  149.8 0.1 maximum_convert_fusion
  149.9 0.3 multiply_convert_fusion.1
  150.2 0.1 copy.44
  150.4 0.3 fusion.78
  150.7 0.4 fusion.23
  151.1 2.0 all-gather
  153.1 0.1 bitcast_add_fusion.4
  153.2 17.9 %all_gather.31 = f32[4,4,64,128]{3,2,1,0:T(8,128)S(1)} all-gather(f32[1,4,64,128]{3,2,1,0:T(8,128)S(1)} %bitcast_add_fusion.4), channel_id=1, replica_groups=mesh['seq_0'=4,'seq_1'=4,'seq_2'=2,'tp'=16] {'seq_1'}, dimensions={0}, use_global_device_ids=true | all-gather | bytes 655360 | tf_op jit(solution)/shard_map/all_gather | solution.py:65
  171.1 0.1 multiply_add_fusion
  171.2 12.4 %all_gather.32 = f32[4,4,64,128]{3,2,1,0:T(8,128)S(1)} all-gather(f32[1,4,64,128]{3,2,1,0:T(8,128)S(1)} %multiply_add_fusion), channel_id=1, replica_groups=mesh['seq_0'=4,'seq_1'=4,'seq_2'=2,'tp'=16] {'seq_0'}, dimensions={0}, use_global_device_ids=true | all-gather | bytes 655360 | tf_op jit(solution)/shard_map/all_gather | solution.py:65
  183.5 3.7 %fusion.14 = f32[512,4,64]{0,2,1:T(8,128)S(1)} fusion(bf16[512,4,64]{0,2,1:T(8,128)(2,1)S(1)} %bitcast.197, f32[4,512]{1,0:T(4,128)S(1)} %get-tuple-element.14, f32[4,512]{1,0:T(4,128)S(1)} %bitcast.202, f32[512,512]{1,0:T(8,128)S(1)} %fusion.78, pred[512,512]{1,0:T(8,128)(4,1)S(1)} %iota_compare_fusion), kind=kOutput, calls=%fused_computation.18 | convolution fusion | flops 810549248 | bytes 2113536 | tf_op jit(solution)/shard_map/hts,shp->thp/dot_general | solution.py:161
  187.2 1.4 fusion.18
  188.6 1.2 copy.48
  189.9 0.0 copy-start.7
  189.9 1.7 multiply_reduce_fusion
  191.6 0.1 broadcast_multiply_fusion
  191.7 16.6 %all_to_all.36 = f32[16,512,4]{1,2,0:T(4,128)S(1)} all-to-all(f32[16,512,4]{1,2,0:T(4,128)S(1)} %broadcast_in_dim.69), channel_id=1, replica_groups=mesh['seq_0'=4,'seq_1'=4,'seq_2'=2,'tp'=16] {'tp'}, dimensions={0} | all-to-all | bytes 262144 | tf_op jit(solution)/shard_map/all_to_all | solution.py:19
  208.3 0.1 multiply_reduce_fusion.1
  208.5 0.5 fusion.13
  208.9 0.5 copy.49
  209.5 27.5 %all_to_all.37 = bf16[16,64,512]{2,1,0:T(8,128)(2,1)S(1)} all-to-all(bf16[16,64,512]{2,1,0:T(8,128)(2,1)S(1)} %bitcast.192), channel_id=1, replica_groups=mesh['seq_0'=4,'seq_1'=4,'seq_2'=2,'tp'=16] {'tp'}, dimensions={0} | all-to-all | bytes 2097152 | tf_op jit(solution)/shard_map/all_to_all | solution.py:77
  237.0 0.1 reduce_sum.72
  237.1 0.1 broadcast_in_dim.70
  237.2 31.4 %all_to_all.38 = bf16[16,64,512]{2,1,0:T(8,128)(2,1)S(1)} all-to-all(bf16[16,64,512]{2,1,0:T(8,128)(2,1)S(1)} %broadcast_in_dim.70), channel_id=1, replica_groups=mesh['seq_0'=4,'seq_1'=4,'seq_2'=2,'tp'=16] {'tp'}, dimensions={0} | all-to-all | bytes 2097152 | tf_op jit(solution)/shard_map/all_to_all | solution.py:19
  268.7 1.2 fusion.19
  (38 shorter events, 0.2 us)
Async XLA Ops:
  0.0 13.2 %copy-start = (bf16[256,1024]{1,0:T(8,128)(2,1)S(1)}, bf16[256,1024]{1,0:T(8,128)(2,1)}, u32[]{:S(2)}) copy-start(bf16[256,1024]{1,0:T(8,128)(2,1)} %param.17) | copy-start | bytes 1572868
  1.8 20.1 %all-to-all-start.1 = ((f32[16,1,512]{2,1,0:T(1,128)}), f32[16,1,512]{2,1,0:T(1,128)S(1)}, u32[]{:S(2)}, u32[]{:S(2)}) async-start(f32[16,1,512]{2,1,0:T(1,128)} %broadcast_in_dim.34), calls=%async_computation.1 | async-start | bytes 65536 | tf_op jit(solution)/shard_map/all_to_all | solution.py:19
  21.9 53.1 %all-to-all-start = ((f32[16,64,512]{2,1,0:T(8,128)}), f32[16,64,512]{2,1,0:T(8,128)S(1)}, u32[]{:S(2)}, u32[]{:S(2)}) async-start(f32[16,64,512]{2,1,0:T(8,128)} %bitcast.2), calls=%async_computation | async-start | bytes 4194304 | tf_op jit(solution)/shard_map/all_to_all | solution.py:33
  75.2 5.4 %copy-start.11 = (f32[4]{0:T(128)S(1)}, f32[4]{0:T(128)}, u32[]{:S(2)}) copy-start(f32[4]{0:T(128)} %param.25) | copy-start | bytes 52
  75.2 5.4 %copy-start.6 = (f32[4,64]{1,0:T(4,128)S(1)}, f32[4,64]{1,0:T(4,128)}, u32[]{:S(2)}) copy-start(f32[4,64]{1,0:T(4,128)} %param.23) | copy-start | bytes 3076
  75.2 5.4 %copy-start.5 = (f32[4,256]{1,0:T(4,128)S(1)}, f32[4,256]{1,0:T(4,128)}, u32[]{:S(2)}) copy-start(f32[4,256]{1,0:T(4,128)} %param.22) | copy-start | bytes 12292
  75.2 32.3 %copy-start.3 = (bf16[1024,64]{0,1:T(8,128)(2,1)S(1)}, bf16[1024,64]{0,1:T(8,128)(2,1)}, u32[]{:S(2)}) copy-start(bf16[1024,64]{0,1:T(8,128)(2,1)} %param.20) | copy-start | bytes 393220
  76.3 33.5 %copy-start.9 = (bf16[1024,256]{1,0:T(8,128)(2,1)S(1)}, bf16[1024,256]{1,0:T(8,128)(2,1)}, u32[]{:S(2)}) copy-start(bf16[1024,256]{1,0:T(8,128)(2,1)} %param.19) | copy-start | bytes 1572868
  76.3 31.2 %all-to-all-start.2 = ((bf16[16,64,512]{2,1,0:T(8,128)(2,1)}), bf16[16,64,512]{2,1,0:T(8,128)(2,1)S(1)}, u32[]{:S(2)}, u32[]{:S(2)}) async-start(bf16[16,64,512]{2,1,0:T(8,128)(2,1)} %broadcast_in_dim.62), calls=%async_computation.2 | async-start | bytes 2097152 | tf_op jit(solution)/shard_map/all_to_all | solution.py:19
  107.9 8.1 %collective-permute-start.1 = (bf16[3,64]{0,1:T(8,128)(2,1)S(1)}, bf16[3,64]{0,1:T(8,128)(2,1)S(1)}, u32[]{:S(2)}, u32[]{:S(2)}) collective-permute-start(bf16[3,64]{0,1:T(8,128)(2,1)S(1)} %slice.182), channel_id=1, source_target_pairs={{0,16},{16,32},{32,48},{48,64},{64,80},{80,96},{96,112},{112,128},... | collective-permute-start | bytes 1160 | tf_op jit(solution)/shard_map/ppermute | solution.py:51
  110.3 11.1 %copy-start.4 = (bf16[1024,4]{0,1:T(4,128)(2,1)S(1)}, bf16[1024,4]{0,1:T(4,128)(2,1)}, u32[]{:S(2)}) copy-start(bf16[1024,4]{0,1:T(4,128)(2,1)} %param.21) | copy-start | bytes 24580
  110.3 11.1 %copy-start.8 = (f32[4]{0:T(128)S(1)}, f32[4]{0:T(128)}, u32[]{:S(2)}) copy-start(f32[4]{0:T(128)} %param.24) | copy-start | bytes 52
  110.4 39.5 %collective-permute-start = (bf16[3,256]{1,0:T(4,128)(2,1)S(1)}, bf16[3,256]{1,0:T(4,128)(2,1)S(1)}, u32[]{:S(2)}, u32[]{:S(2)}) collective-permute-start(bf16[3,256]{1,0:T(4,128)(2,1)S(1)} %slice.177), channel_id=1, source_target_pairs={{0,16},{16,32},{32,48},{48,64},{64,80},{80,96},{96,112},{112,128},... | collective-permute-start | bytes 4616 | tf_op jit(solution)/shard_map/ppermute | solution.py:51
  117.4 33.0 %all-to-all-start.3 = ((bf16[16,512,64]{1,2,0:T(8,128)(2,1)}), bf16[16,512,64]{1,2,0:T(8,128)(2,1)S(1)}, u32[]{:S(2)}, u32[]{:S(2)}) async-start(bf16[16,512,64]{1,2,0:T(8,128)(2,1)} %broadcast_in_dim.63), calls=%async_computation.3 | async-start | bytes 2097152 | tf_op jit(solution)/shard_map/all_to_all | solution.py:19
  183.5 3.7 %copy-start.12 = (f32[4]{0:T(128)S(1)}, f32[4]{0:T(128)}, u32[]{:S(2)}) copy-start(f32[4]{0:T(128)} %param.26) | copy-start | bytes 52
  189.9 18.6 %copy-start.2 = (bf16[256,1024]{1,0:T(8,128)(2,1)S(1)}, bf16[256,1024]{1,0:T(8,128)(2,1)}, u32[]{:S(2)}) copy-start(bf16[256,1024]{1,0:T(8,128)(2,1)} %param.28) | copy-start | bytes 1572868
  189.9 18.5 %copy-start.7 = (f32[256]{0:T(256)S(1)}, f32[256]{0:T(256)}, u32[]{:S(2)}) copy-start(f32[256]{0:T(256)} %param.27) | copy-start | bytes 3076
  237.0 31.7 %copy-start.1 = (bf16[512,256]{1,0:T(8,128)(2,1)S(1)}, bf16[512,256]{1,0:T(8,128)(2,1)}, u32[]{:S(2)}) copy-start(bf16[512,256]{1,0:T(8,128)(2,1)} %param.15) | copy-start | bytes 786436
  237.0 31.7 %copy-start.10 = (bf16[1024,256]{1,0:T(8,128)(2,1)S(1)}, bf16[1024,256]{1,0:T(8,128)(2,1)}, u32[]{:S(2)}) copy-start(bf16[1024,256]{1,0:T(8,128)(2,1)} %param.29) | copy-start | bytes 1572868
where the time goes:
time: 271 us; the launch traced here: 270 us
  blocking collectives  134 us (49%)
  waiting for transfers between devices  82.6 us (30%)
  starting transfers between devices  29.8 us (11%)
  matrix products  11.6 us (4%)
  local copies, waits for them, and re-layouts  7.27 us (3%)
  other arithmetic  4.27 us (2%)
    all_gather x6, blocking collectives, entering(): pieces = jax.tree.map(lambda part: lax.all_gather(part, axis), running)  58.3 us
    all_to_all x1, waiting for transfers between devices, sent_and_summed(): tiles = lax.all_to_all(in_blocks(shard, dim, peers), axis, 0, 0, tiled=True)  49.4 us
    all_to_all x2, blocking collectives, sent_to_all(): return lax.all_to_all(copies, axis, split_axis=0, concat_axis=0, tiled=True)  48.1 us
    all_to_all x3, waiting for transfers between devices, sent_to_all(): return lax.all_to_all(copies, axis, split_axis=0, concat_axis=0, tiled=True)  32.2 us
    all_to_all x1, blocking collectives, summed_on_arrival(): lax.all_to_all(tiles, axis, split_axis=0, concat_axis=0, tiled=True)  27.5 us
    all_to_all x3, starting transfers between devices, sent_to_all(): return lax.all_to_all(copies, axis, split_axis=0, concat_axis=0, tiled=True)  19.6 us
    ppermute x2, starting transfers between devices, shifted(): return lax.ppermute(shard, axis, pairs)  6.51 us
  transfers between devices with their start and end apart: 6, of which 4 were waited for; matrix products, arithmetic and copies ran while one was open for 3% of the time, Pallas kernels for 0%

commit v1 on v0

v1 whole, which is shorter than its diff:
```python
import functools

import jax
import jax.numpy as jnp
from jax import lax
from jax.experimental import pallas as pl
from jax.experimental.pallas import tpu as pltpu
from jax.sharding import Mesh
from jax.sharding import PartitionSpec as P

GROUPS = 4
EPS = 1e-05
SEQ = ("x", "yh", "core")
TP = ("z", "yl")
F32 = jnp.float32
BF16 = jnp.bfloat16
MESH = pl.DeviceIdType.MESH

ORDER = (4, -3, 3, -2, 2, -1, 1, 0)


def nt(a, b):
    return lax.dot_general(a, b, (((1,), (1,)), ((), ())), preferred_element_type=F32)


def nn(a, b):
    return jnp.dot(a, b, preferred_element_type=F32)


def silu(x):
    return x * (1.0 / (1.0 + jnp.exp(-x)))


def split2(x):
    high = x.astype(BF16)
    return high, (x - high.astype(F32)).astype(BF16)


class Copies:
    def __init__(self, send, recv):
        self.send, self.recv, self.used, self.all = send, recv, 0, []

    def make(self, src, dst, **where):
        k = self.used
        self.used += 1
        copy = pltpu.make_async_remote_copy(
            src_ref=src,
            dst_ref=dst,
            send_sem=self.send.at[k],
            recv_sem=self.recv.at[k],
            device_id=where,
            device_id_type=MESH,
        )
        self.all.append(copy)
        return copy

    def go(self, src, dst, **where):
        copy = self.make(src, dst, **where)
        copy.start()
        return copy

    def drain(self):
        for copy in self.all:
            copy.wait_send()
        self.all = []


def reduce_scatter(cp, z, y, nz, pa, pb, ya, ra, la, rb, lb, yb, ysend, hooks):
    at = lambda off: lax.rem(z + off + nz, nz)
    right, left, other = at(1), at(-1), 1 - y
    up = lambda v: v.astype(F32)
    across = {}
    for k, off in enumerate(ORDER):
        across[off] = (k, cp.go(pa.at[at(off), other], ya.at[k], yl=other))
    br = cp.go(pb.at[at(4)], rb.at[0], z=right)
    bl = cp.go(pb.at[at(-3)], lb.at[0], z=left)
    hooks[0]()

    def own(off):
        k, copy = across[off]
        copy.wait_recv()
        return up(pa[at(off), y]) + up(ya[k])

    pa[at(4), y] = own(4).astype(BF16)
    ar = cp.go(pa.at[at(4), y], ra.at[0], z=right)
    pa[at(-3), y] = own(-3).astype(BF16)
    al = cp.go(pa.at[at(-3), y], la.at[0], z=left)
    for s in (1, 2, 3):
        br.wait_recv()
        rb[s - 1] = (up(rb[s - 1]) + up(pb[at(4 - s)])).astype(BF16)
        br = cp.go(rb.at[s - 1], rb.at[s], z=right)
        if s < 3:
            bl.wait_recv()
            lb[s - 1] = (up(lb[s - 1]) + up(pb[at(s - 3)])).astype(BF16)
            bl = cp.go(lb.at[s - 1], lb.at[s], z=left)
        mine = own(4 - s)
        ar.wait_recv()
        ra[s - 1] = (up(ra[s - 1]) + mine).astype(BF16)
        ar = cp.go(ra.at[s - 1], ra.at[s], z=right)
        if s < 3:
            mine = own(s - 3)
            al.wait_recv()
            la[s - 1] = (up(la[s - 1]) + mine).astype(BF16)
            al = cp.go(la.at[s - 1], la.at[s], z=left)
        hooks[s]()
    br.wait_recv()
    bl.wait_recv()
    ysend[...] = (up(pb[z, other]) + up(rb[3, other]) + up(lb[2, other])).astype(BF16)
    by = cp.go(ysend, yb, yl=other)
    mine = own(0)
    ar.wait_recv()
    al.wait_recv()
    total_a = mine + up(ra[3]) + up(la[2])
    total_b = up(pb[z, y]) + up(rb[3, y]) + up(lb[2, y])
    by.wait_recv()
    return total_a, total_b + up(yb[...])


def all_gather(cp, z, y, nz, ga, gb):
    at = lambda off: lax.rem(z + off + nz, nz)
    right, left, other = at(1), at(-1), 1 - y
    by = cp.go(gb.at[z, y], gb.at[z, y], yl=other)
    ar = cp.go(ga.at[z, y], ga.at[z, y], z=right)
    al = cp.go(ga.at[z, y], ga.at[z, y], z=left)
    across = [cp.go(ga.at[z, y], ga.at[z, y], yl=other)]
    by.wait_recv()
    br = cp.go(gb.at[z], gb.at[z], z=right)
    bl = cp.go(gb.at[z], gb.at[z], z=left)
    for s in (1, 2, 3, 4):
        ar.wait_recv()
        block = ga.at[at(-s), y]
        if s < 4:
            ar = cp.go(block, block, z=right)
        across.append(cp.go(block, block, yl=other))
        if s < 4:
            al.wait_recv()
            block = ga.at[at(s), y]
            if s < 3:
                al = cp.go(block, block, z=left)
            across.append(cp.go(block, block, yl=other))
        br.wait_recv()
        if s < 4:
            br = cp.go(gb.at[at(-s)], gb.at[at(-s)], z=right)
            bl.wait_recv()
            if s < 3:
                bl = cp.go(gb.at[at(s)], gb.at[at(s)], z=left)
    for copy in across:
        copy.wait_recv()


def gather_scan(cp, buf, place, peers, axis):
    copies = []
    for o in range(1, peers):
        there = lax.rem(place + o, peers)
        copies.append(cp.go(buf.at[place], buf.at[place], **{axis: there}))
    return copies


def pack(ref, where, state, decay):
    high, low = split2(decay)
    ref[where, pl.ds(0, 128), :] = state.astype(BF16)
    row = lax.broadcasted_iota(jnp.int32, (16, 128), 0)
    tail = jnp.where(row == 0, high.astype(F32), jnp.where(row == 1, low.astype(F32), 0.0))
    ref[where, pl.ds(128, 16), :] = tail.astype(BF16)


def unpack(ref, where):
    tail = ref[where, pl.ds(128, 16), :].astype(F32)
    return ref[where, pl.ds(0, 128), :].astype(F32), tail[0:1] + tail[1:2]


def prefix(buf, place, peers):
    run, decay = jnp.zeros((128, 128), F32), jnp.ones((1, 128), F32)
    before, before_decay = run, decay
    for k in range(peers):
        here = place == k
        before = jnp.where(here, run, before)
        before_decay = jnp.where(here, decay, before_decay)
        state, d = unpack(buf, k)
        run, decay = d * run + state, d * decay
    return before, before_decay, run, decay


def seq_shift(sizes, place, by):
    nx, nyh, ncore = sizes[:3]
    total = nx * nyh * ncore
    there = lax.rem(place + by + total, total)
    return dict(x=there // (nyh * ncore), yh=lax.rem(there // ncore, nyh), core=lax.rem(there, ncore))


def token_rows(v):
    return jnp.concatenate([v[0:1, 128 * c : 128 * c + 128] for c in range(v.shape[1] // 128)], axis=0)


def halves(low, high):
    lane = lax.broadcasted_iota(jnp.int32, (low.shape[0], 128), 1)
    return jnp.where(lane < 64, low, high)


def block_kernel(sizes, names, *args):
    r = dict(zip(names, args))
    nx, nyh, ncore, nz, nyl = sizes
    x, yh, core, z, y = (lax.axis_index(a) for a in ("x", "yh", "core", "z", "yl"))
    other, twin = 1 - y, 1 - core
    hid, pa, pb, ga, gb = r["hid"], r["pa"], r["pb"], r["ga"], r["gb"]
    tokens, width = hid.shape
    ca, rows, rank = pa.shape[3], pa.shape[2], r["down"].shape[1]
    place = (x * nyh + yh) * ncore + core
    at = lambda off: lax.rem(z + off + nz, nz)
    mate = z + 1 - 2 * lax.rem(z, 2)
    cp = Copies(r["send"], r["recv"])

    shares = [(o, c) for o in range(nx) for c in range(ncore) if o or c]
    share_peer = lambda o, c: dict(x=lax.rem(x + o, nx), core=lax.rem(core + c, ncore))
    peers = [dict(z=at(o)) for o in range(1, nz)] + [dict(yl=other), dict(z=mate, yl=other)]
    peers += [dict(yh=lax.rem(yh + o, nyh)) for o in range(1, nyh)]
    peers += [share_peer(o, c) for o, c in shares]
    peers += [seq_shift(sizes, place, 1), seq_shift(sizes, place, -1)]
    barrier = pltpu.get_barrier_semaphore()
    for peer in peers:
        pl.semaphore_signal(barrier, inc=1, device_id=peer, device_id_type=MESH)

    loads = {}
    for k, name in enumerate(("hid", "down", "state_w", "value_w", "step_w", "gate_w", "odown", "oup")):
        loads[name] = pltpu.make_async_copy(r[name + "_h"], r[name], r["load_sem"].at[k])
        loads[name].start()

    loads["hid"].wait()
    loads["down"].wait()
    wide = hid[...].astype(F32)
    ones = jnp.ones((8, width), BF16)
    high, low = split2(wide * wide)
    squares = token_rows(nt(ones, high) + nt(ones, low))
    taps = r["conv_s"][...]
    blank = jnp.zeros_like(taps)
    taps = jnp.where(y == 0, jnp.concatenate([taps, blank], axis=1), jnp.concatenate([blank, taps], axis=1))
    r["q0"][...] = jnp.concatenate([squares, taps], axis=0)
    part = nn((wide * r["gain"][...]).astype(BF16), r["down"][...]).astype(BF16)
    pa[...] = part[:, :ca].reshape(pa.shape)
    pb[...] = part[:, ca:].reshape(pb.shape)
    share = x * ncore + core
    half = r["state_w"].shape[1]
    span = rank // (nx * ncore)
    eye = (lax.broadcasted_iota(jnp.int32, (half, half), 0) == lax.broadcasted_iota(jnp.int32, (half, half), 1)).astype(BF16)
    loads["state_w"].wait()
    gz = r["gz"]
    gz[z] = nt(eye, r["state_w"][pl.ds(pl.multiple_of(share * span, span), span), :]).astype(BF16)
    pl.semaphore_wait(barrier, len(peers))

    picked = z // 2
    held = {}

    def hook0():
        held["q"] = cp.go(r["q0"], r["q1"], yl=other)
        held["gz"] = []
        for o in range(1, nz):
            copy = cp.make(gz.at[z], gz.at[z], z=at(o))
            cp.all.pop()
            sends = at(o) // 2 == lax.rem(z, 4)
            comes = lax.rem(at(-o), 4) == picked
            held["gz"].append((sends, comes, copy))

            @pl.when(sends)
            def _():
                copy.start()

    def hook1():
        held["q"].wait_recv()
        r["qz"][z] = r["q0"][...] + r["q1"][...]
        held["qz"] = [cp.go(r["qz"].at[z], r["qz"].at[z], z=at(o)) for o in range(1, nz)]

    def hook2():
        for sends, comes, copy in held["gz"]:
            @pl.when(comes)
            def _():
                copy.wait_recv()

            @pl.when(sends)
            def _():
                copy.wait_send()

        for k in range(2):
            r["ss"][share, k, y] = gz[4 * k + picked]
        held["ss"] = cp.go(r["ss"].at[share, :, y], r["ss"].at[share, :, y], yl=other)

    def hook3():
        held["ss"].wait_recv()
        held["shares"] = [cp.go(r["ss"].at[share], r["ss"].at[share], **share_peer(o, c)) for o, c in shares]

    total_a, total_b = reduce_scatter(
        cp, z, y, nz, pa, pb, *(r[n] for n in ("ya", "ra", "la", "rb", "lb", "yb", "ysend")), (hook0, hook1, hook2, hook3)
    )
    for copy in held["qz"]:
        copy.wait_recv()
    block = 2 * z + y
    summed = r["qz"][0]
    for k in range(1, nz):
        summed = summed + r["qz"][k]
    row = jnp.zeros((1, 128), F32)
    per = 128 // rows
    for c in range(tokens // 128):
        row = jnp.where(block // per == c, summed[c : c + 1], row)
    wanted = lax.broadcasted_iota(jnp.int32, (rows, 128), 1) == lax.broadcasted_iota(jnp.int32, (rows, 128), 0) + rows * lax.rem(block, per)
    mean = jnp.sum(jnp.where(wanted, row, 0.0), axis=1, keepdims=True) / (width * nz * nyl)
    factor = lax.rsqrt(mean + EPS)
    ga[z, y] = (total_a * factor).astype(BF16)
    gb[z, y] = (total_b * factor).astype(BF16)
    all_gather(cp, z, y, nz, ga, gb)

    last = pl.ds(rows - 16, 16)
    following = seq_shift(sizes, place, 1)
    ha = cp.go(ga.at[nz - 1, 1, last], r["halo_a"], **following)
    hb = cp.go(gb.at[nz - 1, 1, last], r["halo_b"], **following)
    red_a, red_b = ga[...].reshape(tokens, ca), gb[...].reshape(tokens, rank - ca)

    for copy in held["shares"]:
        copy.wait_recv()
    swt = r["swt"]
    for k in range(nx * ncore):
        swt[:, span * k : span * (k + 1)] = r["ss"][k].reshape(2 * nyl * half, span)
    pre = r["pre"]
    chans = 2 * nyl * half
    for name in ("value_w", "step_w", "gate_w"):
        loads[name].wait()
    value_w = r["value_w"]

    def project(a, b):
        values = nn(a, value_w[:ca]) + nn(b, value_w[ca:])
        states = nt(a, swt[:, :ca]) + nt(b, swt[:, ca:])
        return values, states

    pre[16:, :width], pre[16:, width:] = project(red_a, red_b)

    heads = r["step_w"].shape[1]
    put = (lax.broadcasted_iota(jnp.int32, (8, heads), 0) == lax.broadcasted_iota(jnp.int32, (8, heads), 1)).astype(BF16)
    step_t = nt(put, r["step_w"][...]).astype(BF16)
    raw = nt(step_t[:, :ca], red_a) + nt(step_t[:, ca:], red_b)
    head = lax.broadcasted_iota(jnp.int32, (8, 1), 0)
    bias, decay = jnp.zeros((8, 1), F32), jnp.zeros((8, 1), F32)
    for h in range(heads):
        bias = jnp.where(head == h, r["bias"][h], bias)
        decay = jnp.where(head == h, r["decay"][h], decay)
    raw = raw + bias
    step = jnp.maximum(raw, 0.0) + jnp.log1p(jnp.exp(-jnp.abs(raw)))
    lane = lax.broadcasted_iota(jnp.int32, (8, tokens), 1)
    logs = -jnp.exp(decay) * step
    k = 1
    while k < tokens:
        logs = logs + jnp.where(lane >= k, pltpu.roll(logs, k, axis=1), 0.0)
        k *= 2
    final = logs[:, tokens - 1 : tokens]
    ending = jnp.exp(final - logs) * step
    stack = jnp.concatenate([logs, ending, jnp.exp(logs), jnp.zeros((104, tokens), F32)], axis=0)
    cols = r["cols"]
    cols[...] = stack.T
    whole = jnp.exp(final)

    ha.wait_recv()
    hb.wait_recv()
    hv, hs = project(r["halo_a"][...], r["halo_b"][...])
    keep = jnp.where(place == 0, 0.0, 1.0)
    pre[:16, :width] = hv * keep
    pre[:16, width:] = hs * keep
    vact, bact, cact = r["vact"], r["bact"], r["cact"]
    weights = r["conv_v"][...]
    sweights = jnp.concatenate([r["qz"][picked][4:8], r["qz"][4 + picked][4:8]], axis=1)
    for c in range(tokens // 128):
        acc_v = jnp.zeros((128, width), F32)
        acc_s = jnp.zeros((128, chans), F32)
        for t in range(4):
            window = pre[13 + t + 128 * c : 13 + t + 128 * c + 128, :]
            acc_v = acc_v + weights[t : t + 1] * window[:, :width]
            acc_s = acc_s + sweights[t : t + 1] * window[:, width:]
        here = slice(128 * c, 128 * c + 128)
        vact[here] = silu(acc_v).astype(BF16)
        acts = silu(acc_s).astype(BF16)
        bact[here] = acts[:, :128]
        cact[here] = acts[:, 128:]

    eye = (lax.broadcasted_iota(jnp.int32, (128, 128), 0) == lax.broadcasted_iota(jnp.int32, (128, 128), 1)).astype(BF16)
    b_t = nt(eye, bact[...]).astype(BF16)
    own_state, own_decay = [], []
    for p in range(2):
        h = 2 * p
        ends = halves(cols[:, 8 + h : 9 + h], cols[:, 9 + h : 10 + h])
        scaled = (vact[:, 128 * p : 128 * p + 128].astype(F32) * ends).astype(BF16)
        own_state.append(nn(b_t, scaled))
        own_decay.append(halves(whole[h : h + 1], whole[h + 1 : h + 2]))
    theirs = lambda a, b, c: jnp.where(c == 0, a, b)
    one_send, one_recv = r["one"].at[0], r["one"].at[1]
    pack(r["one"], 0, theirs(*own_state, twin), theirs(*own_decay, twin))
    first = cp.go(one_send, one_recv, core=twin)
    mine, mine_decay = theirs(*own_state, core), theirs(*own_decay, core)
    gates = nn(red_a, r["gate_w"][:ca]) + nn(red_b, r["gate_w"][ca:])
    r["gact"][...] = silu(gates)
    first.wait_recv()
    got, got_decay = unpack(r["one"], 1)
    state0, state1 = jnp.where(core == 0, mine, got), jnp.where(core == 0, got, mine)
    decay0, decay1 = jnp.where(core == 0, mine_decay, got_decay), jnp.where(core == 0, got_decay, mine_decay)
    pack(r["two"], yh, decay1 * state0 + state1, decay0 * decay1)
    second = gather_scan(cp, r["two"], yh, nyh, "yh")

    mix = r["mix"]
    for c in range(tokens // 128):
        here = slice(128 * c, 128 * c + 128)
        past = 128 * c + 128
        couple = nt(cact[here], bact[:past])
        seen = lax.broadcasted_iota(jnp.int32, (128, past), 0) + 128 * c >= lax.broadcasted_iota(jnp.int32, (128, past), 1)
        for p in range(2):
            outs = []
            for h in (2 * p, 2 * p + 1):
                spread = cols[here, h : h + 1] - logs[h : h + 1, :past]
                fade = jnp.where(seen, jnp.exp(jnp.minimum(spread, 0.0)), 0.0)
                m = (couple * fade * step[h : h + 1, :past]).astype(BF16)
                outs.append(nn(m, vact[:past, 128 * p : 128 * p + 128]))
            skip = halves(jnp.full((1, 1), r["skip"][2 * p], F32), jnp.full((1, 1), r["skip"][2 * p + 1], F32))
            values = vact[here, 128 * p : 128 * p + 128].astype(F32)
            mix[here, 128 * p : 128 * p + 128] = halves(*outs) + skip * values

    for copy in second:
        copy.wait_recv()
    before, before_decay, run, run_decay = prefix(r["two"], yh, nyh)
    pack(r["three"], x, run, run_decay)
    third = gather_scan(cp, r["three"], x, nx, "x")
    for copy in third:
        copy.wait_recv()
    far = prefix(r["three"], x, nx)[0]
    entry0 = before_decay * far + before
    entry1 = decay0 * entry0 + state0
    inc = r["inc"]
    inc[core] = theirs(entry0, entry1, core).astype(BF16)
    r["fin"][...] = theirs(entry0, entry1, twin).astype(BF16)
    fourth = cp.go(r["fin"], inc.at[core], core=twin)
    fourth.wait_recv()

    gated = []
    for p in range(2):
        h = 2 * p
        carried = nn(cact[...], inc[p]) * halves(cols[:, 16 + h : 17 + h], cols[:, 17 + h : 18 + h])
        gated.append((mix[:, 128 * p : 128 * p + 128] + carried) * r["gact"][:, 128 * p : 128 * p + 128])
    gated = jnp.concatenate(gated, axis=1)
    high, low = split2(gated * gated)
    own = token_rows(nt(ones, high) + nt(ones, low))
    r["gq"][0] = jnp.concatenate([own, jnp.zeros_like(own)], axis=0)
    groups = [
        cp.go(r["gq"].at[0], r["gq"].at[1], yl=other),
        cp.go(r["gq"].at[0], r["gq"].at[2], z=mate),
        cp.go(r["gq"].at[0], r["gq"].at[3], z=mate, yl=other),
    ]
    loads["odown"].wait()
    pf = r["pf"]
    pf[...] = nn((gated * r["gain2"][...]).astype(BF16), r["odown"][...])
    for copy in groups:
        copy.wait_recv()
    squares = r["gq"][0] + r["gq"][1] + r["gq"][2] + r["gq"][3]
    norm = lax.rsqrt(squares / (width * 4) + EPS)
    norm = jnp.concatenate([norm, jnp.zeros((120, 128), F32)], axis=0).T
    per = 128 // (2 * rows)
    pa2, pb2 = r["pa2"], r["pb2"]
    for c in range(tokens // 128):
        scaled = (pf[128 * c : 128 * c + 128, :] * norm[:, c : c + 1]).astype(BF16)
        pa2[per * c : per * c + per] = scaled[:, :ca].reshape(per, *pa2.shape[1:])
        pb2[per * c : per * c + per] = scaled[:, ca:].reshape(per, *pb2.shape[1:])
    nothing = lambda: None
    total_a, total_b = reduce_scatter(
        cp, z, y, nz, pa2, pb2, *(r[n] for n in ("ya2", "ra2", "la2", "rb2", "lb2", "yb2", "ysend2")), (nothing,) * 4
    )
    ga2, gb2 = r["ga2"], r["gb2"]
    ga2[z, y] = total_a.astype(BF16)
    gb2[z, y] = total_b.astype(BF16)
    all_gather(cp, z, y, nz, ga2, gb2)
    loads["oup"].wait()
    oup = r["oup"]
    update = nn(ga2[...].reshape(tokens, ca), oup[:ca]) + nn(gb2[...].reshape(tokens, rank - ca), oup[ca:])
    r["out"][...] = (hid[...].astype(F32) + update).astype(BF16)
    cp.drain()


def on_device(sizes, hidden, norm_gain, rank_down, gate_up, value_up, state_up, step_up, conv_value, conv_state, step_bias, decay_log, skip_gain, gate_gain, out_down, out_up):
    nx, nyh, ncore, nz, nyl = sizes
    tokens, width = hidden.shape
    rank = rank_down.shape[1]
    half = state_up.shape[1]
    rows = tokens // (nz * nyl)
    ca = rank * 5 // 8
    cb = rank - ca
    vm, hbm, sm = (pl.BlockSpec(memory_space=s) for s in (pltpu.VMEM, pl.ANY, pltpu.SMEM))
    operands = [
        ("hid_h", hbm, hidden), ("gain", vm, norm_gain.reshape(1, -1)), ("down_h", hbm, rank_down), ("gate_w_h", hbm, gate_up),
        ("value_w_h", hbm, value_up), ("state_w_h", hbm, state_up), ("step_w_h", hbm, step_up), ("conv_v", vm, conv_value),
        ("conv_s", vm, conv_state), ("bias", sm, step_bias), ("decay", sm, decay_log), ("skip", sm, skip_gain),
        ("gain2", vm, gate_gain.reshape(1, -1)), ("odown_h", hbm, out_down), ("oup_h", hbm, out_up),
    ]
    like = lambda a: pltpu.VMEM(a.shape, a.dtype)
    half_sums = lambda t: [
        ("pa" + t, pltpu.VMEM((nz, 2, rows, ca), BF16)), ("pb" + t, pltpu.VMEM((nz, 2, rows, cb), BF16)),
        ("ya" + t, pltpu.VMEM((nz, rows, ca), BF16)), ("ra" + t, pltpu.VMEM((4, rows, ca), BF16)), ("la" + t, pltpu.VMEM((3, rows, ca), BF16)),
        ("rb" + t, pltpu.VMEM((4, 2, rows, cb), BF16)), ("lb" + t, pltpu.VMEM((3, 2, rows, cb), BF16)),
        ("yb" + t, pltpu.VMEM((rows, cb), BF16)), ("ysend" + t, pltpu.VMEM((rows, cb), BF16)),
        ("ga" + t, pltpu.VMEM((nz, 2, rows, ca), BF16)), ("gb" + t, pltpu.VMEM((nz, 2, rows, cb), BF16)),
    ]
    count = 160
    scratch = [
        ("hid", like(hidden)), ("down", like(rank_down)), ("gate_w", like(gate_up)), ("value_w", like(value_up)), ("state_w", like(state_up)),
        ("step_w", like(step_up)), ("odown", like(out_down)), ("oup", like(out_up)), *half_sums(""), *half_sums("2"),
        ("q0", pltpu.VMEM((8, 128), F32)), ("q1", pltpu.VMEM((8, 128), F32)), ("qz", pltpu.VMEM((nz, 8, 128), F32)),
        ("gz", pltpu.VMEM((nz, half, rank // (nx * ncore)), BF16)), ("ss", pltpu.VMEM((nx * ncore, 2, nyl, half, rank // (nx * ncore)), BF16)),
        ("swt", pltpu.VMEM((2 * nyl * half, rank), BF16)), ("halo_a", pltpu.VMEM((16, ca), BF16)), ("halo_b", pltpu.VMEM((16, cb), BF16)),
        ("pre", pltpu.VMEM((16 + tokens, width + 2 * nyl * half), F32)), ("vact", pltpu.VMEM((tokens, width), BF16)),
        ("bact", pltpu.VMEM((tokens, 128), BF16)), ("cact", pltpu.VMEM((tokens, 128), BF16)), ("gact", pltpu.VMEM((tokens, width), F32)),
        ("cols", pltpu.VMEM((tokens, 128), F32)), ("mix", pltpu.VMEM((tokens, width), F32)), ("pf", pltpu.VMEM((tokens, rank), F32)),
        ("one", pltpu.VMEM((2, 144, 128), BF16)), ("two", pltpu.VMEM((nyh, 144, 128), BF16)), ("three", pltpu.VMEM((nx, 144, 128), BF16)),
        ("fin", pltpu.VMEM((128, 128), BF16)), ("inc", pltpu.VMEM((2, 128, 128), BF16)), ("gq", pltpu.VMEM((4, 8, 128), F32)),
        ("send", pltpu.SemaphoreType.DMA((count,))), ("recv", pltpu.SemaphoreType.DMA((count,))), ("load_sem", pltpu.SemaphoreType.DMA((8,))),
    ]
    names = [n for n, _, _ in operands] + ["out"] + [n for n, _ in scratch]
    return pl.pallas_call(
        functools.partial(block_kernel, sizes, names),
        out_shape=jax.ShapeDtypeStruct(hidden.shape, BF16),
        in_specs=[s for _, s, _ in operands],
        out_specs=vm,
        scratch_shapes=[s for _, s in scratch],
        compiler_params=pltpu.CompilerParams(collective_id=0, has_side_effects=True, vmem_limit_bytes=60 * 2**20),
    )(*(a for _, _, a in operands))


def grid_sizes(mesh):
    seq, tp = mesh.shape["seq"], mesh.shape["tp"]
    nx = nyh = 1
    if seq == 32:
        nx = nyh = 4
    return (nx, nyh, 2, tp // 2, 2)


def solution(mesh):
    sizes = grid_sizes(mesh)
    finer = Mesh(mesh.devices.reshape(sizes), SEQ + TP)
    rows, cols, flat = P(TP, None), P(None, TP), P(TP)
    placed = (P(SEQ, TP), flat, rows, cols, cols, cols, cols, cols, cols, flat, flat, flat, flat, rows, cols)
    return jax.shard_map(
        functools.partial(on_device, sizes), mesh=finer, in_specs=placed, out_specs=P(SEQ, TP), check_vma=False
    )
```

time: 271 us -> 116 us (0.43)
  the two profiles are of different devices: /device:TPU:2 before, /device:TPU:8 now
where the time goes in v1:
time: 116 us; the launch traced here: 115 us
  Pallas kernels  111 us (96%)
  local copies, waits for them, and re-layouts  4.3 us (4%)
    pallas_call x1, Pallas kernels, on_device(): pl.pallas_call(functools.partial(block_kernel, sizes, names), out_shape=j...  111 us
    unnamed x5, local copies, waits for them, and re-layouts  4.3 us

profile of v1, /device:TPU:8, one launch (start us, length us, event | category | flops | bytes accessed | tf_op | source)
XLA Modules:
  0.0 115.5 jit_solution(8039383045999528030)
XLA Ops:
  0.0 0.0 copy-start
  0.0 1.8 %copy.16.args_5_ = bf16[1024,64]{1,0:T(8,128)(2,1)} copy(bf16[1024,64]{0,1:T(8,128)(2,1)} %param.20) | data formatting | bytes 262144 | tf_op args[5]
  1.8 0.0 copy-done
  1.8 0.9 copy.17.args_6_
  2.6 111.2 %shard_map.145 = bf16[512,256]{1,0:T(8,128)(2,1)} custom-call(bf16[512,256]{1,0:T(8,128)(2,1)} %args_0_.4, f32[1,256]{1,0:T(1,128)} %bitcast.2, bf16[256,1024]{1,0:T(8,128)(2,1)} %args_2_.4, bf16[1024,256]{1,0:T(8,128)(2,1)} %args_3_.4, bf16[1024,256]{1,0:T(8,128)(2,1)} %args_4_.4, bf16[1024,64]{1,0:T(8,128)(2,1)} %copy.16.args_5_, ...), custom_call_target="tpu_custom_call" | custom-call | tf_op jit(solution)/shard_map/pallas_call | solution.py:517
  113.8 1.7 %copy.19 = bf16[512,256]{1,0:T(8,128)(2,1)} copy(bf16[512,256]{1,0:T(8,128)(2,1)} %shard_map.145) | data formatting | bytes 524288
Async XLA Ops:
  0.0 1.8 %copy-start = (bf16[1024,4]{0,1:T(4,128)(2,1)S(1)}, bf16[1024,4]{0,1:T(4,128)(2,1)}, u32[]{:S(2)}) copy-start(bf16[1024,4]{0,1:T(4,128)(2,1)} %param.21) | copy-start | bytes 24580

commit v2 on v1

--- a/solution.py
+++ b/solution.py
@@ -16,7 +16,9 @@
 BF16 = jnp.bfloat16
 MESH = pl.DeviceIdType.MESH
 
-ORDER = (4, -3, 3, -2, 2, -1, 1, 0)
+ORDER = (3, -3, 4, 2, -2, 1, -1, 0)
+SKIP = (True, True)
+PARTS = (("y", 256), ("y", 256), ("y", 256), ("z", 256))
 
 
 def nt(a, b):
@@ -65,92 +67,168 @@
         self.all = []
 
 
-def reduce_scatter(cp, z, y, nz, pa, pb, ya, ra, la, rb, lb, yb, ysend, hooks):
+def up(v):
+    return v.astype(F32)
+
+
+def flow_y_first(cp, env, buf, scale, factor, done):
+    z, y, nz = env
     at = lambda off: lax.rem(z + off + nz, nz)
-    right, left, other = at(1), at(-1), 1 - y
-    up = lambda v: v.astype(F32)
-    across = {}
+    other = 1 - y
+    p, yr, r, h, g = buf["p"], buf["y"], buf["r"], buf["h"], buf["g"]
+    part = {1: pl.ds(0, 16), -1: pl.ds(16, 16)}
+    across, got = {}, {}
     for k, off in enumerate(ORDER):
-        across[off] = (k, cp.go(pa.at[at(off), other], ya.at[k], yl=other))
-    br = cp.go(pb.at[at(4)], rb.at[0], z=right)
-    bl = cp.go(pb.at[at(-3)], lb.at[0], z=left)
-    hooks[0]()
+        across[off] = (k, cp.go(p.at[at(off), other], yr.at[k], yl=other))
+        if k == 2:
+            yield
+    yield
 
     def own(off):
         k, copy = across[off]
         copy.wait_recv()
-        return up(pa[at(off), y]) + up(ya[k])
-
-    pa[at(4), y] = own(4).astype(BF16)
-    ar = cp.go(pa.at[at(4), y], ra.at[0], z=right)
-    pa[at(-3), y] = own(-3).astype(BF16)
-    al = cp.go(pa.at[at(-3), y], la.at[0], z=left)
-    for s in (1, 2, 3):
-        br.wait_recv()
-        rb[s - 1] = (up(rb[s - 1]) + up(pb[at(4 - s)])).astype(BF16)
-        br = cp.go(rb.at[s - 1], rb.at[s], z=right)
-        if s < 3:
-            bl.wait_recv()
-            lb[s - 1] = (up(lb[s - 1]) + up(pb[at(s - 3)])).astype(BF16)
-            bl = cp.go(lb.at[s - 1], lb.at[s], z=left)
-        mine = own(4 - s)
-        ar.wait_recv()
-        ra[s - 1] = (up(ra[s - 1]) + mine).astype(BF16)
-        ar = cp.go(ra.at[s - 1], ra.at[s], z=right)
-        if s < 3:
-            mine = own(s - 3)
-            al.wait_recv()
-            la[s - 1] = (up(la[s - 1]) + mine).astype(BF16)
-            al = cp.go(la.at[s - 1], la.at[s], z=left)
-        hooks[s]()
-    br.wait_recv()
-    bl.wait_recv()
-    ysend[...] = (up(pb[z, other]) + up(rb[3, other]) + up(lb[2, other])).astype(BF16)
-    by = cp.go(ysend, yb, yl=other)
-    mine = own(0)
-    ar.wait_recv()
-    al.wait_recv()
-    total_a = mine + up(ra[3]) + up(la[2])
-    total_b = up(pb[z, y]) + up(rb[3, y]) + up(lb[2, y])
-    by.wait_recv()
-    return total_a, total_b + up(yb[...])
-
-
-def all_gather(cp, z, y, nz, ga, gb):
+        sums = up(p[at(off), y]) + up(yr[k])
+        return sums if scale is None else sums * scale[at(off), y][:, :1]
+
+    for d, s in ((0, 1), (1, -1)):
+        p[at(3 * s), y] = own(3 * s).astype(BF16)
+        got[s, 3] = cp.go(p.at[at(3 * s), y], r.at[d, 0], z=at(s))
+    p[at(4), y] = own(4).astype(BF16)
+    for s in (1, -1):
+        got[s, 4] = cp.go(p.at[at(4), y, part[s]], h.at[part[s]], z=at(2 * s))
+    yield
+    far = 2 if SKIP[0] else 1
+    for d, s in ((0, 1), (1, -1)):
+        mine = own(2 * s)
+        got[s, 3].wait_recv()
+        got[s, 4].wait_recv()
+        r[d, 0] = (up(r[d, 0]) + mine).astype(BF16)
+        r[d, 0, part[s]] = (up(r[d, 0, part[s]]) + up(h[part[s]])).astype(BF16)
+        got[s, 2] = cp.go(r.at[d, 0], r.at[d, 1], z=at(far * s))
+        if SKIP[0]:
+            p[at(s), y] = own(s).astype(BF16)
+            got[s, 1] = cp.go(p.at[at(s), y], r.at[d, 2], z=at(s))
+    yield
+    if not SKIP[0]:
+        for d, s in ((0, 1), (1, -1)):
+            mine = own(s)
+            got[s, 2].wait_recv()
+            r[d, 1] = (up(r[d, 1]) + mine).astype(BF16)
+            got[s, 1] = cp.go(r.at[d, 1], r.at[d, 2], z=at(s))
+        yield
+    total = own(0)
+    for d, s in ((0, 1), (1, -1)):
+        for e in (1, 2) if SKIP[0] else (2,):
+            got[s, 3 - e].wait_recv()
+            total = total + up(r[d, e])
+    if factor is not None:
+        total = total * factor()[y]
+    mine = g.at[z, y]
+    g[z, y] = total.astype(BF16)
+    seen = {}
+    for hop in (1, 2) if SKIP[1] else (1,):
+        for s in (1, -1):
+            seen[s, hop] = cp.go(mine, mine, z=at(hop * s))
+    last = [cp.go(mine, mine, yl=other)]
+    yield
+    for k in (1, 2, 3):
+        for s in (1, -1):
+            seen[s, k].wait_recv()
+            block = g.at[at(-k * s), y]
+            if k == 1 and not SKIP[1]:
+                seen[s, 2] = cp.go(block, block, z=at(s))
+            if k == 2:
+                half = g.at[at(-2 * s), y, part[s]]
+                seen[s, 4] = cp.go(half, half, z=at(2 * s))
+                seen[s, 3] = cp.go(block, block, z=at(s))
+            last.append(cp.go(block, block, yl=other))
+        yield
+    for s in (1, -1):
+        seen[s, 4].wait_recv()
+        half = g.at[at(4), y, part[s]]
+        last.append(cp.go(half, half, yl=other))
+    yield
+    for copy in last:
+        copy.wait_recv()
+    done()
+
+
+def flow_z_first(cp, env, buf, scale, factor, done):
+    z, y, nz = env
     at = lambda off: lax.rem(z + off + nz, nz)
-    right, left, other = at(1), at(-1), 1 - y
-    by = cp.go(gb.at[z, y], gb.at[z, y], yl=other)
-    ar = cp.go(ga.at[z, y], ga.at[z, y], z=right)
-    al = cp.go(ga.at[z, y], ga.at[z, y], z=left)
-    across = [cp.go(ga.at[z, y], ga.at[z, y], yl=other)]
-    by.wait_recv()
-    br = cp.go(gb.at[z], gb.at[z], z=right)
-    bl = cp.go(gb.at[z], gb.at[z], z=left)
-    for s in (1, 2, 3, 4):
-        ar.wait_recv()
-        block = ga.at[at(-s), y]
-        if s < 4:
-            ar = cp.go(block, block, z=right)
-        across.append(cp.go(block, block, yl=other))
-        if s < 4:
-            al.wait_recv()
-            block = ga.at[at(s), y]
-            if s < 3:
-                al = cp.go(block, block, z=left)
-            across.append(cp.go(block, block, yl=other))
-        br.wait_recv()
-        if s < 4:
-            br = cp.go(gb.at[at(-s)], gb.at[at(-s)], z=right)
-            bl.wait_recv()
-            if s < 3:
-                bl = cp.go(gb.at[at(s)], gb.at[at(s)], z=left)
-    for copy in across:
-        copy.wait_recv()
+    p, yr, r, h, g = buf["p"], buf["y"], buf["r"], buf["h"], buf["g"]
+    part = {1: pl.ds(0, 16), -1: pl.ds(16, 16)}
+    every = slice(None)
+    got, seen = {}, {}
+    for d, s in ((0, 1), (1, -1)):
+        got[s, 3] = cp.go(p.at[at(3 * s)], r.at[d, 0], z=at(s))
+        got[s, 4] = cp.go(p.at[at(4), :, part[s]], h.at[:, part[s]], z=at(2 * s))
+    yield
+    far = 2 if SKIP[0] else 1
+    for d, s in ((0, 1), (1, -1)):
+        got[s, 3].wait_recv()
+        got[s, 4].wait_recv()
+        r[d, 0] = (up(r[d, 0]) + up(p[at(2 * s)])).astype(BF16)
+        r[d, 0, :, part[s]] = (up(r[d, 0, :, part[s]]) + up(h[:, part[s]])).astype(BF16)
+        got[s, 2] = cp.go(r.at[d, 0], r.at[d, 1], z=at(far * s))
+        if SKIP[0]:
+            got[s, 1] = cp.go(p.at[at(s)], r.at[d, 2], z=at(s))
+    yield
+    if not SKIP[0]:
+        for d, s in ((0, 1), (1, -1)):
+            got[s, 2].wait_recv()
+            r[d, 1] = (up(r[d, 1]) + up(p[at(s)])).astype(BF16)
+            got[s, 1] = cp.go(r.at[d, 1], r.at[d, 2], z=at(s))
+        yield
+    total = up(p[z])
+    for d, s in ((0, 1), (1, -1)):
+        for e in (1, 2) if SKIP[0] else (2,):
+            got[s, 3 - e].wait_recv()
+            total = total + up(r[d, e])
+    yr[0] = total.astype(BF16)
+    swap = cp.go(yr.at[0], yr.at[1], yl=1 - y)
+    yield
+    swap.wait_recv()
+    total = up(yr[0]) + up(yr[1])
+    if factor is not None:
+        total = total * factor()[...]
+    g[z] = total.astype(BF16)
+    for hop in (1, 2) if SKIP[1] else (1,):
+        for s in (1, -1):
+            seen[s, hop] = cp.go(g.at[z], g.at[z], z=at(hop * s))
+    yield
+    for k in (1, 2, 3):
+        for s in (1, -1):
+            seen[s, k].wait_recv()
+            block = g.at[at(-k * s)]
+            if k == 1 and not SKIP[1]:
+                seen[s, 2] = cp.go(block, block, z=at(s))
+            if k == 2:
+                half = g.at[at(-2 * s), :, part[s]]
+                seen[s, 4] = cp.go(half, half, z=at(2 * s))
+                seen[s, 3] = cp.go(block, block, z=at(s))
+        yield
+    for s in (1, -1):
+        seen[s, 4].wait_recv()
+    done()
+
+
+def run_flows(flows, hooks):
+    turn = 0
+    while flows:
+        left = []
+        for flow in flows:
+            if next(flow, flow) is not flow:
+                left.append(flow)
+        flows = left
+        if turn < len(hooks):
+            hooks[turn]()
+        turn += 1
 
 
 def gather_scan(cp, buf, place, peers, axis):
     copies = []
-    for o in range(1, peers):
+    for o in sorted(range(1, peers), key=lambda o: -min(o, peers - o)):
         there = lax.rem(place + o, peers)
         copies.append(cp.go(buf.at[place], buf.at[place], **{axis: there}))
     return copies
@@ -181,6 +259,37 @@
     return before, before_decay, run, decay
 
 
+FLOWS = {"y": flow_y_first, "z": flow_z_first}
+
+
+class Column:
+    def __init__(self, ref):
+        self.ref = ref
+
+    def __getitem__(self, k):
+        return self.ref[k][..., :1]
+
+
+def group_buffers(side, nz, rows):
+    out = []
+    for i, (order, c) in enumerate(PARTS):
+        both = (2, rows, c) if order == "z" else (rows, c)
+        shapes = dict(p=(nz, 2, rows, c), g=(nz, 2, rows, c), r=(2, 3, *both), h=both, y=(2, *both) if order == "z" else (nz, *both))
+        if side == "in":
+            shapes["halo"] = (16, c)
+        out += [(f"{side}{i}{k}", pltpu.VMEM(v, BF16)) for k, v in shapes.items()]
+    return out
+
+
+def split_groups(r, side):
+    out, start = [], 0
+    for i, (order, c) in enumerate(PARTS):
+        g = {k: r[f"{side}{i}{k}"] for k in ("p", "g", "r", "h", "y", "halo") if f"{side}{i}{k}" in r}
+        out.append(dict(g, order=order, cols=slice(start, start + c)))
+        start += c
+    return out
+
+
 def seq_shift(sizes, place, by):
     nx, nyh, ncore = sizes[:3]
     total = nx * nyh * ncore
@@ -202,9 +311,10 @@
     nx, nyh, ncore, nz, nyl = sizes
     x, yh, core, z, y = (lax.axis_index(a) for a in ("x", "yh", "core", "z", "yl"))
     other, twin = 1 - y, 1 - core
-    hid, pa, pb, ga, gb = r["hid"], r["pa"], r["pb"], r["ga"], r["gb"]
+    hid, groups_in, groups_out = r["hid"], split_groups(r, "in"), split_groups(r, "out")
     tokens, width = hid.shape
-    ca, rows, rank = pa.shape[3], pa.shape[2], r["down"].shape[1]
+    rows, rank = groups_in[0]["p"].shape[2], r["down"].shape[1]
+    env = (z, y, nz)
     place = (x * nyh + yh) * ncore + core
     at = lambda off: lax.rem(z + off + nz, nz)
     mate = z + 1 - 2 * lax.rem(z, 2)
@@ -236,19 +346,19 @@
     taps = jnp.where(y == 0, jnp.concatenate([taps, blank], axis=1), jnp.concatenate([blank, taps], axis=1))
     r["q0"][...] = jnp.concatenate([squares, taps], axis=0)
     part = nn((wide * r["gain"][...]).astype(BF16), r["down"][...]).astype(BF16)
-    pa[...] = part[:, :ca].reshape(pa.shape)
-    pb[...] = part[:, ca:].reshape(pb.shape)
+    for g in groups_in:
+        g["p"][...] = part[:, g["cols"]].reshape(g["p"].shape)
     share = x * ncore + core
-    half = r["state_w"].shape[1]
+    half = r["state_w"].shape[0]
     span = rank // (nx * ncore)
-    eye = (lax.broadcasted_iota(jnp.int32, (half, half), 0) == lax.broadcasted_iota(jnp.int32, (half, half), 1)).astype(BF16)
     loads["state_w"].wait()
     gz = r["gz"]
-    gz[z] = nt(eye, r["state_w"][pl.ds(pl.multiple_of(share * span, span), span), :]).astype(BF16)
+    gz[z] = r["state_w"][:, pl.ds(pl.multiple_of(share * span, span), span)]
     pl.semaphore_wait(barrier, len(peers))
 
     picked = z // 2
     held = {}
+    nothing = lambda: None
 
     def hook0():
         held["q"] = cp.go(r["q0"], r["q1"], yl=other)
@@ -287,31 +397,38 @@
         held["ss"].wait_recv()
         held["shares"] = [cp.go(r["ss"].at[share], r["ss"].at[share], **share_peer(o, c)) for o, c in shares]
 
-    total_a, total_b = reduce_scatter(
-        cp, z, y, nz, pa, pb, *(r[n] for n in ("ya", "ra", "la", "rb", "lb", "yb", "ysend")), (hook0, hook1, hook2, hook3)
-    )
-    for copy in held["qz"]:
-        copy.wait_recv()
-    block = 2 * z + y
-    summed = r["qz"][0]
-    for k in range(1, nz):
-        summed = summed + r["qz"][k]
-    row = jnp.zeros((1, 128), F32)
-    per = 128 // rows
-    for c in range(tokens // 128):
-        row = jnp.where(block // per == c, summed[c : c + 1], row)
-    wanted = lax.broadcasted_iota(jnp.int32, (rows, 128), 1) == lax.broadcasted_iota(jnp.int32, (rows, 128), 0) + rows * lax.rem(block, per)
-    mean = jnp.sum(jnp.where(wanted, row, 0.0), axis=1, keepdims=True) / (width * nz * nyl)
-    factor = lax.rsqrt(mean + EPS)
-    ga[z, y] = (total_a * factor).astype(BF16)
-    gb[z, y] = (total_b * factor).astype(BF16)
-    all_gather(cp, z, y, nz, ga, gb)
+    fac = r["fac"]
+
+    def factor():
+        if "factor" not in held:
+            held["factor"] = True
+            for copy in held["qz"]:
+                copy.wait_recv()
+            summed = r["qz"][0]
+            for k in range(1, nz):
+                summed = summed + r["qz"][k]
+            near = 2 * rows
+            per = 128 // near
+            row = jnp.zeros((1, 128), F32)
+            for c in range(tokens // 128):
+                row = jnp.where(z // per == c, summed[c : c + 1], row)
+            wanted = lax.broadcasted_iota(jnp.int32, (near, 128), 1) == lax.broadcasted_iota(jnp.int32, (near, 128), 0) + near * lax.rem(z, per)
+            mean = jnp.sum(jnp.where(wanted, row, 0.0), axis=1, keepdims=True) / (width * nz * nyl)
+            fac[...] = jnp.broadcast_to(lax.rsqrt(mean + EPS), (near, 128)).reshape(2, rows, 128)
+        return Column(fac)
+
+    flows = [FLOWS[g["order"]](cp, env, g, None, factor, nothing) for g in groups_in]
+    for flow, g in zip(flows, groups_in):
+        if g["order"] == "y":
+            next(flow)
+    run_flows(flows, (hook0, hook1, hook2, hook3))
 
     last = pl.ds(rows - 16, 16)
     following = seq_shift(sizes, place, 1)
-    ha = cp.go(ga.at[nz - 1, 1, last], r["halo_a"], **following)
-    hb = cp.go(gb.at[nz - 1, 1, last], r["halo_b"], **following)
-    red_a, red_b = ga[...].reshape(tokens, ca), gb[...].reshape(tokens, rank - ca)
+    halos = [cp.go(g["g"].at[nz - 1, 1, last], g["halo"], **following) for g in groups_in]
+    reds = [g["g"][...].reshape(tokens, -1) for g in groups_in]
+    cuts = [g["cols"] for g in groups_in]
+    over = lambda f, blocks, take: sum(f(b, take(c)) for b, c in zip(blocks, cuts))
 
     for copy in held["shares"]:
         copy.wait_recv()
@@ -324,17 +441,14 @@
         loads[name].wait()
     value_w = r["value_w"]
 
-    def project(a, b):
-        values = nn(a, value_w[:ca]) + nn(b, value_w[ca:])
-        states = nt(a, swt[:, :ca]) + nt(b, swt[:, ca:])
-        return values, states
-
-    pre[16:, :width], pre[16:, width:] = project(red_a, red_b)
-
-    heads = r["step_w"].shape[1]
-    put = (lax.broadcasted_iota(jnp.int32, (8, heads), 0) == lax.broadcasted_iota(jnp.int32, (8, heads), 1)).astype(BF16)
-    step_t = nt(put, r["step_w"][...]).astype(BF16)
-    raw = nt(step_t[:, :ca], red_a) + nt(step_t[:, ca:], red_b)
+    def project(blocks):
+        return over(nn, blocks, lambda c: value_w[c]), over(nt, blocks, lambda c: swt[:, c])
+
+    pre[16:, :width], pre[16:, width:] = project(reds)
+
+    heads = r["step_w"].shape[0]
+    step_t = jnp.concatenate([r["step_w"][...].astype(F32), jnp.zeros((8 - heads, rank), F32)], axis=0).astype(BF16)
+    raw = over(lambda b, w: nt(w, b), reds, lambda c: step_t[:, c])
     head = lax.broadcasted_iota(jnp.int32, (8, 1), 0)
     bias, decay = jnp.zeros((8, 1), F32), jnp.zeros((8, 1), F32)
     for h in range(heads):
@@ -355,16 +469,13 @@
     cols[...] = stack.T
     whole = jnp.exp(final)
 
-    ha.wait_recv()
-    hb.wait_recv()
-    hv, hs = project(r["halo_a"][...], r["halo_b"][...])
-    keep = jnp.where(place == 0, 0.0, 1.0)
-    pre[:16, :width] = hv * keep
-    pre[:16, width:] = hs * keep
+    gates = over(nn, reds, lambda c: r["gate_w"][c])
+    r["gact"][...] = silu(gates)
     vact, bact, cact = r["vact"], r["bact"], r["cact"]
     weights = r["conv_v"][...]
     sweights = jnp.concatenate([r["qz"][picked][4:8], r["qz"][4 + picked][4:8]], axis=1)
-    for c in range(tokens // 128):
+
+    def convolve(c):
         acc_v = jnp.zeros((128, width), F32)
         acc_s = jnp.zeros((128, chans), F32)
         for t in range(4):
@@ -376,6 +487,16 @@
         acts = silu(acc_s).astype(BF16)
         bact[here] = acts[:, :128]
         cact[here] = acts[:, 128:]
+
+    for c in range(1, tokens // 128):
+        convolve(c)
+    for copy in halos:
+        copy.wait_recv()
+    hv, hs = project([g["halo"][...] for g in groups_in])
+    keep = jnp.where(place == 0, 0.0, 1.0)
+    pre[:16, :width] = hv * keep
+    pre[:16, width:] = hs * keep
+    convolve(0)
 
     eye = (lax.broadcasted_iota(jnp.int32, (128, 128), 0) == lax.broadcasted_iota(jnp.int32, (128, 128), 1)).astype(BF16)
     b_t = nt(eye, bact[...]).astype(BF16)
@@ -391,8 +512,6 @@
     pack(r["one"], 0, theirs(*own_state, twin), theirs(*own_decay, twin))
     first = cp.go(one_send, one_recv, core=twin)
     mine, mine_decay = theirs(*own_state, core), theirs(*own_decay, core)
-    gates = nn(red_a, r["gate_w"][:ca]) + nn(red_b, r["gate_w"][ca:])
-    r["gact"][...] = silu(gates)
     first.wait_recv()
     got, got_decay = unpack(r["one"], 1)
     state0, state1 = jnp.where(core == 0, mine, got), jnp.where(core == 0, got, mine)
@@ -450,28 +569,33 @@
     loads["odown"].wait()
     pf = r["pf"]
     pf[...] = nn((gated * r["gain2"][...]).astype(BF16), r["odown"][...])
+    nrm = r["nrm"]
+    for g in groups_out:
+        if g["order"] == "y":
+            g["p"][...] = pf[:, g["cols"]].astype(BF16).reshape(g["p"].shape)
+    early = [FLOWS["y"](cp, env, g, nrm, None, nothing) for g in groups_out if g["order"] == "y"]
+    for flow in early + early:
+        next(flow)
     for copy in groups:
         copy.wait_recv()
     squares = r["gq"][0] + r["gq"][1] + r["gq"][2] + r["gq"][3]
     norm = lax.rsqrt(squares / (width * 4) + EPS)
     norm = jnp.concatenate([norm, jnp.zeros((120, 128), F32)], axis=0).T
     per = 128 // (2 * rows)
-    pa2, pb2 = r["pa2"], r["pb2"]
     for c in range(tokens // 128):
-        scaled = (pf[128 * c : 128 * c + 128, :] * norm[:, c : c + 1]).astype(BF16)
-        pa2[per * c : per * c + per] = scaled[:, :ca].reshape(per, *pa2.shape[1:])
-        pb2[per * c : per * c + per] = scaled[:, ca:].reshape(per, *pb2.shape[1:])
-    nothing = lambda: None
-    total_a, total_b = reduce_scatter(
-        cp, z, y, nz, pa2, pb2, *(r[n] for n in ("ya2", "ra2", "la2", "rb2", "lb2", "yb2", "ysend2")), (nothing,) * 4
-    )
-    ga2, gb2 = r["ga2"], r["gb2"]
-    ga2[z, y] = total_a.astype(BF16)
-    gb2[z, y] = total_b.astype(BF16)
-    all_gather(cp, z, y, nz, ga2, gb2)
+        by_row = jnp.broadcast_to(norm[:, c : c + 1], (128, 128))
+        nrm[per * c : per * c + per] = by_row.reshape(per, 2, rows, 128)
+        for g in groups_out:
+            if g["order"] == "z":
+                scaled = (pf[128 * c : 128 * c + 128, g["cols"]] * by_row[:, :1]).astype(BF16)
+                g["p"][per * c : per * c + per] = scaled.reshape(per, *g["p"].shape[1:])
+    late = [FLOWS["z"](cp, env, g, None, None, nothing) for g in groups_out if g["order"] == "z"]
+    for flow in late:
+        next(flow)
+    run_flows(late + early, ())
     loads["oup"].wait()
     oup = r["oup"]
-    update = nn(ga2[...].reshape(tokens, ca), oup[:ca]) + nn(gb2[...].reshape(tokens, rank - ca), oup[ca:])
+    update = over(nn, [g["g"][...].reshape(tokens, -1) for g in groups_out], lambda c: oup[c])
     r["out"][...] = (hid[...].astype(F32) + update).astype(BF16)
     cp.drain()
 
@@ -482,33 +606,25 @@
     rank = rank_down.shape[1]
     half = state_up.shape[1]
     rows = tokens // (nz * nyl)
-    ca = rank * 5 // 8
-    cb = rank - ca
     vm, hbm, sm = (pl.BlockSpec(memory_space=s) for s in (pltpu.VMEM, pl.ANY, pltpu.SMEM))
     operands = [
         ("hid_h", hbm, hidden), ("gain", vm, norm_gain.reshape(1, -1)), ("down_h", hbm, rank_down), ("gate_w_h", hbm, gate_up),
-        ("value_w_h", hbm, value_up), ("state_w_h", hbm, state_up), ("step_w_h", hbm, step_up), ("conv_v", vm, conv_value),
+        ("value_w_h", hbm, value_up), ("state_w_h", hbm, state_up.T), ("step_w_h", hbm, step_up.T), ("conv_v", vm, conv_value),
         ("conv_s", vm, conv_state), ("bias", sm, step_bias), ("decay", sm, decay_log), ("skip", sm, skip_gain),
         ("gain2", vm, gate_gain.reshape(1, -1)), ("odown_h", hbm, out_down), ("oup_h", hbm, out_up),
     ]
     like = lambda a: pltpu.VMEM(a.shape, a.dtype)
-    half_sums = lambda t: [
-        ("pa" + t, pltpu.VMEM((nz, 2, rows, ca), BF16)), ("pb" + t, pltpu.VMEM((nz, 2, rows, cb), BF16)),
-        ("ya" + t, pltpu.VMEM((nz, rows, ca), BF16)), ("ra" + t, pltpu.VMEM((4, rows, ca), BF16)), ("la" + t, pltpu.VMEM((3, rows, ca), BF16)),
-        ("rb" + t, pltpu.VMEM((4, 2, rows, cb), BF16)), ("lb" + t, pltpu.VMEM((3, 2, rows, cb), BF16)),
-        ("yb" + t, pltpu.VMEM((rows, cb), BF16)), ("ysend" + t, pltpu.VMEM((rows, cb), BF16)),
-        ("ga" + t, pltpu.VMEM((nz, 2, rows, ca), BF16)), ("gb" + t, pltpu.VMEM((nz, 2, rows, cb), BF16)),
-    ]
-    count = 160
+    count = 400
     scratch = [
-        ("hid", like(hidden)), ("down", like(rank_down)), ("gate_w", like(gate_up)), ("value_w", like(value_up)), ("state_w", like(state_up)),
-        ("step_w", like(step_up)), ("odown", like(out_down)), ("oup", like(out_up)), *half_sums(""), *half_sums("2"),
+        ("hid", like(hidden)), ("down", like(rank_down)), ("gate_w", like(gate_up)), ("value_w", like(value_up)), ("state_w", like(state_up.T)),
+        ("step_w", like(step_up.T)), ("odown", like(out_down)), ("oup", like(out_up)), *group_buffers("in", nz, rows), *group_buffers("out", nz, rows),
         ("q0", pltpu.VMEM((8, 128), F32)), ("q1", pltpu.VMEM((8, 128), F32)), ("qz", pltpu.VMEM((nz, 8, 128), F32)),
         ("gz", pltpu.VMEM((nz, half, rank // (nx * ncore)), BF16)), ("ss", pltpu.VMEM((nx * ncore, 2, nyl, half, rank // (nx * ncore)), BF16)),
-        ("swt", pltpu.VMEM((2 * nyl * half, rank), BF16)), ("halo_a", pltpu.VMEM((16, ca), BF16)), ("halo_b", pltpu.VMEM((16, cb), BF16)),
+        ("swt", pltpu.VMEM((2 * nyl * half, rank), BF16)), ("fac", pltpu.VMEM((2, rows, 128), F32)),
         ("pre", pltpu.VMEM((16 + tokens, width + 2 * nyl * half), F32)), ("vact", pltpu.VMEM((tokens, width), BF16)),
         ("bact", pltpu.VMEM((tokens, 128), BF16)), ("cact", pltpu.VMEM((tokens, 128), BF16)), ("gact", pltpu.VMEM((tokens, width), F32)),
         ("cols", pltpu.VMEM((tokens, 128), F32)), ("mix", pltpu.VMEM((tokens, width), F32)), ("pf", pltpu.VMEM((tokens, rank), F32)),
+        ("nrm", pltpu.VMEM((nz, 2, rows, 128), F32)),
         ("one", pltpu.VMEM((2, 144, 128), BF16)), ("two", pltpu.VMEM((nyh, 144, 128), BF16)), ("three", pltpu.VMEM((nx, 144, 128), BF16)),
         ("fin", pltpu.VMEM((128, 128), BF16)), ("inc", pltpu.VMEM((2, 128, 128), BF16)), ("gq", pltpu.VMEM((4, 8, 128), F32)),
         ("send", pltpu.SemaphoreType.DMA((count,))), ("recv", pltpu.SemaphoreType.DMA((count,))), ("load_sem", pltpu.SemaphoreType.DMA((8,))),

time: 116 us -> 101 us (0.87)
  Pallas kernels: 111 us -> 99.5 us
  local copies, waits for them, and re-layouts: 4.3 us -> 1.67 us
    pallas_call x1, Pallas kernels: 111 us -> 99.5 us  [on_device(): pl.pallas_call(functools.partial(block_kernel, sizes, names), out_shape=j...]
    unnamed x5 -> x1, local copies, waits for them, and re-layouts: 4.3 us -> 1.67 us
where the time goes in v2:
time: 101 us
  Pallas kernels  99.5 us (99%)
  local copies, waits for them, and re-layouts  1.67 us (2%)
    pallas_call x1, Pallas kernels, on_device(): pl.pallas_call(functools.partial(block_kernel, sizes, names), out_shape=j...  99.5 us

profile of v2, /device:TPU:8, one launch (start us, length us, event | category | flops | bytes accessed | tf_op | source)
XLA Modules:
  0.0 101.2 jit_solution(8619929380738465001)
XLA Ops:
  0.0 99.5 %shard_map.145 = bf16[512,256]{1,0:T(8,128)(2,1)} custom-call(bf16[512,256]{1,0:T(8,128)(2,1)} %args_0_.4, f32[1,256]{1,0:T(1,128)} %bitcast.6, bf16[256,1024]{1,0:T(8,128)(2,1)} %args_2_.4, bf16[1024,256]{1,0:T(8,128)(2,1)} %args_3_.4, bf16[1024,256]{1,0:T(8,128)(2,1)} %args_4_.4, bf16[64,1024]{1,0:T(8,128)(2,1)} %bitcast.4, bf16[4,1024]{1,0:T(4,128)(2,1)} %bitcast.5, ...), custom_call_target="tpu_custom_call" | custom-call | tf_op jit(solution)/shard_map/pallas_call | solution.py:633
  99.5 1.7 %copy.17 = bf16[512,256]{1,0:T(8,128)(2,1)} copy(bf16[512,256]{1,0:T(8,128)(2,1)} %shard_map.145) | data formatting | bytes 524288

commit v3 on v2

--- a/solution.py
+++ b/solution.py
@@ -18,6 +18,7 @@
 
 ORDER = (3, -3, 4, 2, -2, 1, -1, 0)
 SKIP = (True, True)
+EARLY = 3
 PARTS = (("y", 256), ("y", 256), ("y", 256), ("z", 256))
 
 
@@ -78,10 +79,14 @@
     p, yr, r, h, g = buf["p"], buf["y"], buf["r"], buf["h"], buf["g"]
     part = {1: pl.ds(0, 16), -1: pl.ds(16, 16)}
     across, got = {}, {}
-    for k, off in enumerate(ORDER):
-        across[off] = (k, cp.go(p.at[at(off), other], yr.at[k], yl=other))
-        if k == 2:
-            yield
+    def cross(first, last):
+        for k in range(first, last):
+            off = ORDER[k]
+            across[off] = (k, cp.go(p.at[at(off), other], yr.at[k], yl=other))
+
+    cross(0, 3)
+    yield
+    cross(3, EARLY)
     yield
 
     def own(off):
@@ -96,6 +101,7 @@
     p[at(4), y] = own(4).astype(BF16)
     for s in (1, -1):
         got[s, 4] = cp.go(p.at[at(4), y, part[s]], h.at[part[s]], z=at(2 * s))
+    cross(EARLY, len(ORDER))
     yield
     far = 2 if SKIP[0] else 1
     for d, s in ((0, 1), (1, -1)):
@@ -163,6 +169,9 @@
     for d, s in ((0, 1), (1, -1)):
         got[s, 3] = cp.go(p.at[at(3 * s)], r.at[d, 0], z=at(s))
         got[s, 4] = cp.go(p.at[at(4), :, part[s]], h.at[:, part[s]], z=at(2 * s))
+    if SKIP[0]:
+        for d, s in ((0, 1), (1, -1)):
+            got[s, 1] = cp.go(p.at[at(s)], r.at[d, 2], z=at(s))
     yield
     far = 2 if SKIP[0] else 1
     for d, s in ((0, 1), (1, -1)):
@@ -171,8 +180,6 @@
         r[d, 0] = (up(r[d, 0]) + up(p[at(2 * s)])).astype(BF16)
         r[d, 0, :, part[s]] = (up(r[d, 0, :, part[s]]) + up(h[:, part[s]])).astype(BF16)
         got[s, 2] = cp.go(r.at[d, 0], r.at[d, 1], z=at(far * s))
-        if SKIP[0]:
-            got[s, 1] = cp.go(p.at[at(s)], r.at[d, 2], z=at(s))
     yield
     if not SKIP[0]:
         for d, s in ((0, 1), (1, -1)):
@@ -216,14 +223,13 @@
 def run_flows(flows, hooks):
     turn = 0
     while flows:
+        hooks[turn]() if turn < len(hooks) else None
+        turn += 1
         left = []
         for flow in flows:
             if next(flow, flow) is not flow:
                 left.append(flow)
         flows = left
-        if turn < len(hooks):
-            hooks[turn]()
-        turn += 1
 
 
 def gather_scan(cp, buf, place, peers, axis):
@@ -333,10 +339,13 @@
     loads = {}
     for k, name in enumerate(("hid", "down", "state_w", "value_w", "step_w", "gate_w", "odown", "oup")):
         loads[name] = pltpu.make_async_copy(r[name + "_h"], r[name], r["load_sem"].at[k])
-        loads[name].start()
+        if k < 2:
+            loads[name].start()
 
     loads["hid"].wait()
     loads["down"].wait()
+    for name in ("state_w", "value_w", "step_w", "gate_w", "odown", "oup"):
+        loads[name].start()
     wide = hid[...].astype(F32)
     ones = jnp.ones((8, width), BF16)
     high, low = split2(wide * wide)
@@ -417,11 +426,10 @@
             fac[...] = jnp.broadcast_to(lax.rsqrt(mean + EPS), (near, 128)).reshape(2, rows, 128)
         return Column(fac)
 
-    flows = [FLOWS[g["order"]](cp, env, g, None, factor, nothing) for g in groups_in]
-    for flow, g in zip(flows, groups_in):
-        if g["order"] == "y":
-            next(flow)
-    run_flows(flows, (hook0, hook1, hook2, hook3))
+    flows = {o: [FLOWS[o](cp, env, g, None, factor, nothing) for g in groups_in if g["order"] == o] for o in "zy"}
+    for flow in flows["z"] + flows["y"] + flows["y"]:
+        next(flow)
+    run_flows(flows["y"] + flows["z"], (hook0, hook1, hook2, hook3))
 
     last = pl.ds(rows - 16, 16)
     following = seq_shift(sizes, place, 1)
@@ -464,13 +472,11 @@
         k *= 2
     final = logs[:, tokens - 1 : tokens]
     ending = jnp.exp(final - logs) * step
-    stack = jnp.concatenate([logs, ending, jnp.exp(logs), jnp.zeros((104, tokens), F32)], axis=0)
+    stack = jnp.concatenate([logs, ending, jnp.exp(logs), jnp.zeros((8, tokens), F32)], axis=0)
     cols = r["cols"]
     cols[...] = stack.T
     whole = jnp.exp(final)
 
-    gates = over(nn, reds, lambda c: r["gate_w"][c])
-    r["gact"][...] = silu(gates)
     vact, bact, cact = r["vact"], r["bact"], r["cact"]
     weights = r["conv_v"][...]
     sweights = jnp.concatenate([r["qz"][picked][4:8], r["qz"][4 + picked][4:8]], axis=1)
@@ -519,6 +525,8 @@
     pack(r["two"], yh, decay1 * state0 + state1, decay0 * decay1)
     second = gather_scan(cp, r["two"], yh, nyh, "yh")
 
+    gates = over(nn, reds, lambda c: r["gate_w"][c])
+    r["gact"][...] = silu(gates)
     mix = r["mix"]
     for c in range(tokens // 128):
         here = slice(128 * c, 128 * c + 128)
@@ -574,7 +582,7 @@
         if g["order"] == "y":
             g["p"][...] = pf[:, g["cols"]].astype(BF16).reshape(g["p"].shape)
     early = [FLOWS["y"](cp, env, g, nrm, None, nothing) for g in groups_out if g["order"] == "y"]
-    for flow in early + early:
+    for flow in early:
         next(flow)
     for copy in groups:
         copy.wait_recv()
@@ -590,13 +598,13 @@
                 scaled = (pf[128 * c : 128 * c + 128, g["cols"]] * by_row[:, :1]).astype(BF16)
                 g["p"][per * c : per * c + per] = scaled.reshape(per, *g["p"].shape[1:])
     late = [FLOWS["z"](cp, env, g, None, None, nothing) for g in groups_out if g["order"] == "z"]
-    for flow in late:
+    for flow in late + early:
         next(flow)
-    run_flows(late + early, ())
+    run_flows(early + late, ())
     loads["oup"].wait()
     oup = r["oup"]
     update = over(nn, [g["g"][...].reshape(tokens, -1) for g in groups_out], lambda c: oup[c])
-    r["out"][...] = (hid[...].astype(F32) + update).astype(BF16)
+    r["out"][...] = update
     cp.drain()
 
 
@@ -623,21 +631,22 @@
         ("swt", pltpu.VMEM((2 * nyl * half, rank), BF16)), ("fac", pltpu.VMEM((2, rows, 128), F32)),
         ("pre", pltpu.VMEM((16 + tokens, width + 2 * nyl * half), F32)), ("vact", pltpu.VMEM((tokens, width), BF16)),
         ("bact", pltpu.VMEM((tokens, 128), BF16)), ("cact", pltpu.VMEM((tokens, 128), BF16)), ("gact", pltpu.VMEM((tokens, width), F32)),
-        ("cols", pltpu.VMEM((tokens, 128), F32)), ("mix", pltpu.VMEM((tokens, width), F32)), ("pf", pltpu.VMEM((tokens, rank), F32)),
+        ("cols", pltpu.VMEM((tokens, 32), F32)), ("mix", pltpu.VMEM((tokens, width), F32)), ("pf", pltpu.VMEM((tokens, rank), F32)),
         ("nrm", pltpu.VMEM((nz, 2, rows, 128), F32)),
         ("one", pltpu.VMEM((2, 144, 128), BF16)), ("two", pltpu.VMEM((nyh, 144, 128), BF16)), ("three", pltpu.VMEM((nx, 144, 128), BF16)),
         ("fin", pltpu.VMEM((128, 128), BF16)), ("inc", pltpu.VMEM((2, 128, 128), BF16)), ("gq", pltpu.VMEM((4, 8, 128), F32)),
         ("send", pltpu.SemaphoreType.DMA((count,))), ("recv", pltpu.SemaphoreType.DMA((count,))), ("load_sem", pltpu.SemaphoreType.DMA((8,))),
     ]
     names = [n for n, _, _ in operands] + ["out"] + [n for n, _ in scratch]
-    return pl.pallas_call(
+    update = pl.pallas_call(
         functools.partial(block_kernel, sizes, names),
-        out_shape=jax.ShapeDtypeStruct(hidden.shape, BF16),
+        out_shape=jax.ShapeDtypeStruct(hidden.shape, F32),
         in_specs=[s for _, s, _ in operands],
         out_specs=vm,
         scratch_shapes=[s for _, s in scratch],
         compiler_params=pltpu.CompilerParams(collective_id=0, has_side_effects=True, vmem_limit_bytes=60 * 2**20),
     )(*(a for _, _, a in operands))
+    return (hidden.astype(F32) + update).astype(BF16)
 
 
 def grid_sizes(mesh):

time: 101 us -> 96.3 us (0.953)
  Pallas kernels: 99.5 us -> 94.2 us
  other arithmetic: 0 us -> 1.8 us
  local copies, waits for them, and re-layouts: 1.67 us -> 0.01 us
    pallas_call x1, Pallas kernels: 99.5 us -> 94.2 us  [on_device(): pl.pallas_call(functools.partial(block_kernel, sizes, names), out_shape=j...]
    convert_element_type x0 -> x1, other arithmetic: none -> 1.8 us  [on_device(): return (hidden.astype(F32) + update).astype(BF16)]
    unnamed x1 -> x2, local copies, waits for them, and re-layouts: 1.67 us -> 0.01 us
where the time goes in v3:
time: 96.3 us; the launch traced here: 96.1 us
  Pallas kernels  94.2 us (98%)
  other arithmetic  1.8 us (2%)
    pallas_call x1, Pallas kernels, on_device(): pl.pallas_call(functools.partial(block_kernel, sizes, names), out_shape=j...  94.2 us

profile of v3, /device:TPU:8, one launch (start us, length us, event | category | flops | bytes accessed | tf_op | source)
XLA Modules:
  0.0 96.1 jit_solution(9870233437390623688)
XLA Ops:
  0.0 0.0 copy-start
  0.0 94.2 %shard_map.145 = f32[512,256]{1,0:T(8,128)} custom-call(bf16[512,256]{1,0:T(8,128)(2,1)} %args_0_.4, f32[1,256]{1,0:T(1,128)} %bitcast.6, bf16[256,1024]{1,0:T(8,128)(2,1)} %args_2_.4, bf16[1024,256]{1,0:T(8,128)(2,1)} %args_3_.4, bf16[1024,256]{1,0:T(8,128)(2,1)} %args_4_.4, bf16[64,1024]{1,0:T(8,128)(2,1)} %bitcast.4, bf16[4,1024]{1,0:T(4,128)(2,1)} %bitcast.5, ...), custom_call_target="tpu_custom_call" | custom-call | tf_op jit(solution)/shard_map/pallas_call | solution.py:641
  94.2 0.0 copy-done
  94.3 1.8 %add_convert_fusion = bf16[512,256]{1,0:T(8,128)(2,1)} fusion(f32[512,256]{1,0:T(8,128)} %shard_map.145, bf16[512,256]{1,0:T(8,128)(2,1)S(1)} %copy-done), kind=kLoop, calls=%fused_computation | loop fusion | flops 393216 | bytes 1048576 | tf_op jit(solution)/shard_map/convert_element_type | solution.py:649
Async XLA Ops:
  0.0 94.2 %copy-start = (bf16[512,256]{1,0:T(8,128)(2,1)S(1)}, bf16[512,256]{1,0:T(8,128)(2,1)}, u32[]{:S(2)}) copy-start(bf16[512,256]{1,0:T(8,128)(2,1)} %args_0_.4) | copy-start | bytes 786436

commit v4 on v3

--- a/solution.py
+++ b/solution.py
@@ -18,6 +18,7 @@
 
 ORDER = (3, -3, 4, 2, -2, 1, -1, 0)
 SKIP = (True, True)
+SKIP_Z = (True, True)
 EARLY = 3
 PARTS = (("y", 256), ("y", 256), ("y", 256), ("z", 256))
 
@@ -41,31 +42,39 @@
 
 class Copies:
     def __init__(self, send, recv):
-        self.send, self.recv, self.used, self.all = send, recv, 0, []
-
-    def make(self, src, dst, **where):
-        k = self.used
+        self.send, self.recv, self.sent, self.used = send, recv, 0, 0
+        self.free, self.all, self.old = [], [], []
+
+    def hold(self, src, dst, **where):
+        if self.free:
+            self.slot = self.free.pop()
+        else:
+            self.slot, self.sent = self.sent, self.sent + 1
         self.used += 1
-        copy = pltpu.make_async_remote_copy(
+        return pltpu.make_async_remote_copy(
             src_ref=src,
             dst_ref=dst,
-            send_sem=self.send.at[k],
-            recv_sem=self.recv.at[k],
+            send_sem=self.send.at[self.slot],
+            recv_sem=self.recv.at[self.used - 1],
             device_id=where,
             device_id_type=MESH,
         )
-        self.all.append(copy)
+
+    def go(self, src, dst, **where):
+        copy = self.hold(src, dst, **where)
+        copy.start()
+        self.all.append((copy, self.slot))
         return copy
 
-    def go(self, src, dst, **where):
-        copy = self.make(src, dst, **where)
-        copy.start()
-        return copy
+    def turn(self):
+        for copy, slot in self.old:
+            copy.wait_send()
+            self.free.append(slot)
+        self.old, self.all = self.all, []
 
     def drain(self):
-        for copy in self.all:
-            copy.wait_send()
-        self.all = []
+        self.turn()
+        self.turn()
 
 
 def up(v):
@@ -167,13 +176,13 @@
     every = slice(None)
     got, seen = {}, {}
     for d, s in ((0, 1), (1, -1)):
+        got[s, 4] = cp.go(p.at[at(4), :, part[s]], h.at[:, part[s]], z=at(2 * s))
         got[s, 3] = cp.go(p.at[at(3 * s)], r.at[d, 0], z=at(s))
-        got[s, 4] = cp.go(p.at[at(4), :, part[s]], h.at[:, part[s]], z=at(2 * s))
-    if SKIP[0]:
+    if SKIP_Z[0]:
         for d, s in ((0, 1), (1, -1)):
             got[s, 1] = cp.go(p.at[at(s)], r.at[d, 2], z=at(s))
     yield
-    far = 2 if SKIP[0] else 1
+    far = 2 if SKIP_Z[0] else 1
     for d, s in ((0, 1), (1, -1)):
         got[s, 3].wait_recv()
         got[s, 4].wait_recv()
@@ -181,7 +190,7 @@
         r[d, 0, :, part[s]] = (up(r[d, 0, :, part[s]]) + up(h[:, part[s]])).astype(BF16)
         got[s, 2] = cp.go(r.at[d, 0], r.at[d, 1], z=at(far * s))
     yield
-    if not SKIP[0]:
+    if not SKIP_Z[0]:
         for d, s in ((0, 1), (1, -1)):
             got[s, 2].wait_recv()
             r[d, 1] = (up(r[d, 1]) + up(p[at(s)])).astype(BF16)
@@ -189,7 +198,7 @@
         yield
     total = up(p[z])
     for d, s in ((0, 1), (1, -1)):
-        for e in (1, 2) if SKIP[0] else (2,):
+        for e in (1, 2) if SKIP_Z[0] else (2,):
             got[s, 3 - e].wait_recv()
             total = total + up(r[d, e])
     yr[0] = total.astype(BF16)
@@ -200,7 +209,7 @@
     if factor is not None:
         total = total * factor()[...]
     g[z] = total.astype(BF16)
-    for hop in (1, 2) if SKIP[1] else (1,):
+    for hop in (1, 2) if SKIP_Z[1] else (1,):
         for s in (1, -1):
             seen[s, hop] = cp.go(g.at[z], g.at[z], z=at(hop * s))
     yield
@@ -208,7 +217,7 @@
         for s in (1, -1):
             seen[s, k].wait_recv()
             block = g.at[at(-k * s)]
-            if k == 1 and not SKIP[1]:
+            if k == 1 and not SKIP_Z[1]:
                 seen[s, 2] = cp.go(block, block, z=at(s))
             if k == 2:
                 half = g.at[at(-2 * s), :, part[s]]
@@ -220,9 +229,10 @@
     done()
 
 
-def run_flows(flows, hooks):
+def run_flows(cp, flows, hooks):
     turn = 0
     while flows:
+        cp.turn()
         hooks[turn]() if turn < len(hooks) else None
         turn += 1
         left = []
@@ -373,8 +383,7 @@
         held["q"] = cp.go(r["q0"], r["q1"], yl=other)
         held["gz"] = []
         for o in range(1, nz):
-            copy = cp.make(gz.at[z], gz.at[z], z=at(o))
-            cp.all.pop()
+            copy = cp.hold(gz.at[z], gz.at[z], z=at(o))
             sends = at(o) // 2 == lax.rem(z, 4)
             comes = lax.rem(at(-o), 4) == picked
             held["gz"].append((sends, comes, copy))
@@ -426,10 +435,24 @@
             fac[...] = jnp.broadcast_to(lax.rsqrt(mean + EPS), (near, 128)).reshape(2, rows, 128)
         return Column(fac)
 
-    flows = {o: [FLOWS[o](cp, env, g, None, factor, nothing) for g in groups_in if g["order"] == o] for o in "zy"}
+    value_w = r["value_w"]
+    pre = r["pre"]
+    gact = r["gact"]
+
+    def begin(g):
+        block = g["g"][...].reshape(tokens, -1)
+        if "begun" not in held:
+            held["begun"] = True
+            for name in ("value_w", "step_w", "gate_w"):
+                loads[name].wait()
+            pre[16:, :width] = nn(block, value_w[g["cols"]])
+        else:
+            pre[16:, :width] += nn(block, value_w[g["cols"]])
+
+    flows = {o: [FLOWS[o](cp, env, g, None, factor, functools.partial(begin, g) if o == "z" else nothing) for g in groups_in if g["order"] == o] for o in "zy"}
     for flow in flows["z"] + flows["y"] + flows["y"]:
         next(flow)
-    run_flows(flows["y"] + flows["z"], (hook0, hook1, hook2, hook3))
+    run_flows(cp, flows["y"] + flows["z"], (hook0, hook1, hook2, hook3))
 
     last = pl.ds(rows - 16, 16)
     following = seq_shift(sizes, place, 1)
@@ -445,14 +468,13 @@
         swt[:, span * k : span * (k + 1)] = r["ss"][k].reshape(2 * nyl * half, span)
     pre = r["pre"]
     chans = 2 * nyl * half
-    for name in ("value_w", "step_w", "gate_w"):
-        loads[name].wait()
     value_w = r["value_w"]
 
     def project(blocks):
         return over(nn, blocks, lambda c: value_w[c]), over(nt, blocks, lambda c: swt[:, c])
 
-    pre[16:, :width], pre[16:, width:] = project(reds)
+    pre[16:, :width] += sum(nn(b, value_w[g["cols"]]) for b, g in zip(reds, groups_in) if g["order"] == "y")
+    pre[16:, width:] = over(nt, reds, lambda c: swt[:, c])
 
     heads = r["step_w"].shape[0]
     step_t = jnp.concatenate([r["step_w"][...].astype(F32), jnp.zeros((8 - heads, rank), F32)], axis=0).astype(BF16)
@@ -544,6 +566,7 @@
             values = vact[here, 128 * p : 128 * p + 128].astype(F32)
             mix[here, 128 * p : 128 * p + 128] = halves(*outs) + skip * values
 
+    cp.drain()
     for copy in second:
         copy.wait_recv()
     before, before_decay, run, run_decay = prefix(r["two"], yh, nyh)
@@ -597,14 +620,21 @@
             if g["order"] == "z":
                 scaled = (pf[128 * c : 128 * c + 128, g["cols"]] * by_row[:, :1]).astype(BF16)
                 g["p"][per * c : per * c + per] = scaled.reshape(per, *g["p"].shape[1:])
-    late = [FLOWS["z"](cp, env, g, None, None, nothing) for g in groups_out if g["order"] == "z"]
+    def finish(g):
+        if "oup" not in held:
+            held["oup"] = True
+            loads["oup"].wait()
+            r["out"][...] = nn(g["g"][...].reshape(tokens, -1), r["oup"][g["cols"]])
+        else:
+            r["out"][...] += nn(g["g"][...].reshape(tokens, -1), r["oup"][g["cols"]])
+
+    late = [FLOWS["z"](cp, env, g, None, None, functools.partial(finish, g)) for g in groups_out if g["order"] == "z"]
     for flow in late + early:
         next(flow)
-    run_flows(early + late, ())
-    loads["oup"].wait()
+    run_flows(cp, early + late, ())
+    crossing = [g for g in groups_out if g["order"] == "y"]
     oup = r["oup"]
-    update = over(nn, [g["g"][...].reshape(tokens, -1) for g in groups_out], lambda c: oup[c])
-    r["out"][...] = update
+    r["out"][...] += sum(nn(g["g"][...].reshape(tokens, -1), oup[g["cols"]]) for g in crossing)
     cp.drain()
 
 
@@ -622,7 +652,7 @@
         ("gain2", vm, gate_gain.reshape(1, -1)), ("odown_h", hbm, out_down), ("oup_h", hbm, out_up),
     ]
     like = lambda a: pltpu.VMEM(a.shape, a.dtype)
-    count = 400
+    sends, arrivals = 58, 270
     scratch = [
         ("hid", like(hidden)), ("down", like(rank_down)), ("gate_w", like(gate_up)), ("value_w", like(value_up)), ("state_w", like(state_up.T)),
         ("step_w", like(step_up.T)), ("odown", like(out_down)), ("oup", like(out_up)), *group_buffers("in", nz, rows), *group_buffers("out", nz, rows),
@@ -635,7 +665,7 @@
         ("nrm", pltpu.VMEM((nz, 2, rows, 128), F32)),
         ("one", pltpu.VMEM((2, 144, 128), BF16)), ("two", pltpu.VMEM((nyh, 144, 128), BF16)), ("three", pltpu.VMEM((nx, 144, 128), BF16)),
         ("fin", pltpu.VMEM((128, 128), BF16)), ("inc", pltpu.VMEM((2, 128, 128), BF16)), ("gq", pltpu.VMEM((4, 8, 128), F32)),
-        ("send", pltpu.SemaphoreType.DMA((count,))), ("recv", pltpu.SemaphoreType.DMA((count,))), ("load_sem", pltpu.SemaphoreType.DMA((8,))),
+        ("send", pltpu.SemaphoreType.DMA((sends,))), ("recv", pltpu.SemaphoreType.DMA((arrivals,))), ("load_sem", pltpu.SemaphoreType.DMA((8,))),
     ]
     names = [n for n, _, _ in operands] + ["out"] + [n for n, _ in scratch]
     update = pl.pallas_call(

time: 96.3 us -> 91.2 us (0.947)
  Pallas kernels: 94.2 us -> 89.2 us
    pallas_call x1, Pallas kernels: 94.2 us -> 89.2 us  [on_device(): pl.pallas_call(functools.partial(block_kernel, sizes, names), out_shape=j...]
where the time goes in v4:
time: 91.2 us; the launch traced here: 91 us
  Pallas kernels  89.2 us (98%)
  other arithmetic  1.8 us (2%)
    pallas_call x1, Pallas kernels, on_device(): pl.pallas_call(functools.partial(block_kernel, sizes, names), out_shape=j...  89.2 us

profile of v4, /device:TPU:8, one launch (start us, length us, event | category | flops | bytes accessed | tf_op | source)
XLA Modules:
  0.0 91.0 jit_solution(3119318079907880468)
XLA Ops:
  0.0 0.0 copy-start
  0.0 89.2 %shard_map.145 = f32[512,256]{1,0:T(8,128)} custom-call(bf16[512,256]{1,0:T(8,128)(2,1)} %args_0_.4, f32[1,256]{1,0:T(1,128)} %bitcast.6, bf16[256,1024]{1,0:T(8,128)(2,1)} %args_2_.4, bf16[1024,256]{1,0:T(8,128)(2,1)} %args_3_.4, bf16[1024,256]{1,0:T(8,128)(2,1)} %args_4_.4, bf16[64,1024]{1,0:T(8,128)(2,1)} %bitcast.4, bf16[4,1024]{1,0:T(4,128)(2,1)} %bitcast.5, ...), custom_call_target="tpu_custom_call" | custom-call | tf_op jit(solution)/shard_map/pallas_call | solution.py:671
  89.2 0.0 copy-done
  89.2 1.8 %add_convert_fusion = bf16[512,256]{1,0:T(8,128)(2,1)} fusion(f32[512,256]{1,0:T(8,128)} %shard_map.145, bf16[512,256]{1,0:T(8,128)(2,1)S(1)} %copy-done), kind=kLoop, calls=%fused_computation | loop fusion | flops 393216 | bytes 1048576 | tf_op jit(solution)/shard_map/convert_element_type | solution.py:679
Async XLA Ops:
  0.0 89.2 %copy-start = (bf16[512,256]{1,0:T(8,128)(2,1)S(1)}, bf16[512,256]{1,0:T(8,128)(2,1)}, u32[]{:S(2)}) copy-start(bf16[512,256]{1,0:T(8,128)(2,1)} %args_0_.4) | copy-start | bytes 786436

commit v5 on v4

--- a/solution.py
+++ b/solution.py
@@ -624,9 +624,9 @@
         if "oup" not in held:
             held["oup"] = True
             loads["oup"].wait()
-            r["out"][...] = nn(g["g"][...].reshape(tokens, -1), r["oup"][g["cols"]])
+            r["pf"][:, :width] = nn(g["g"][...].reshape(tokens, -1), r["oup"][g["cols"]])
         else:
-            r["out"][...] += nn(g["g"][...].reshape(tokens, -1), r["oup"][g["cols"]])
+            r["pf"][:, :width] += nn(g["g"][...].reshape(tokens, -1), r["oup"][g["cols"]])
 
     late = [FLOWS["z"](cp, env, g, None, None, functools.partial(finish, g)) for g in groups_out if g["order"] == "z"]
     for flow in late + early:
@@ -634,7 +634,8 @@
     run_flows(cp, early + late, ())
     crossing = [g for g in groups_out if g["order"] == "y"]
     oup = r["oup"]
-    r["out"][...] += sum(nn(g["g"][...].reshape(tokens, -1), oup[g["cols"]]) for g in crossing)
+    update = pf[:, :width] + sum(nn(g["g"][...].reshape(tokens, -1), oup[g["cols"]]) for g in crossing)
+    r["out"][...] = update.astype(BF16)
     cp.drain()
 
 
@@ -670,13 +671,13 @@
     names = [n for n, _, _ in operands] + ["out"] + [n for n, _ in scratch]
     update = pl.pallas_call(
         functools.partial(block_kernel, sizes, names),
-        out_shape=jax.ShapeDtypeStruct(hidden.shape, F32),
+        out_shape=jax.ShapeDtypeStruct(hidden.shape, BF16),
         in_specs=[s for _, s, _ in operands],
         out_specs=vm,
         scratch_shapes=[s for _, s in scratch],
         compiler_params=pltpu.CompilerParams(collective_id=0, has_side_effects=True, vmem_limit_bytes=60 * 2**20),
     )(*(a for _, _, a in operands))
-    return (hidden.astype(F32) + update).astype(BF16)
+    return (hidden.astype(F32) + update.astype(F32)).astype(BF16)
 
 
 def grid_sizes(mesh):

time: 91.2 us -> 91 us (level)
  no operation moved by 1% of the time
where the time goes in v5:
time: 91 us; the launch traced here: 90.8 us
  Pallas kernels  89.1 us (98%)
  other arithmetic  1.72 us (2%)
    pallas_call x1, Pallas kernels, on_device(): pl.pallas_call(functools.partial(block_kernel, sizes, names), out_shape=j...  89.1 us

profile of v5, /device:TPU:8, one launch (start us, length us, event | category | flops | bytes accessed | tf_op | source)
XLA Modules:
  0.0 90.8 jit_solution(8883724650678689123)
XLA Ops:
  0.0 0.0 copy-start
  0.0 89.1 %shard_map.145 = bf16[512,256]{1,0:T(8,128)(2,1)} custom-call(bf16[512,256]{1,0:T(8,128)(2,1)} %args_0_.4, f32[1,256]{1,0:T(1,128)} %bitcast.6, bf16[256,1024]{1,0:T(8,128)(2,1)} %args_2_.4, bf16[1024,256]{1,0:T(8,128)(2,1)} %args_3_.4, bf16[1024,256]{1,0:T(8,128)(2,1)} %args_4_.4, bf16[64,1024]{1,0:T(8,128)(2,1)} %bitcast.4, bf16[4,1024]{1,0:T(4,128)(2,1)} %bitcast.5, ...), custom_call_target="tpu_custom_call" | custom-call | tf_op jit(solution)/shard_map/pallas_call | solution.py:672
  89.1 0.0 copy-done
  89.1 1.7 %add_convert_fusion = bf16[512,256]{1,0:T(8,128)(2,1)} fusion(bf16[512,256]{1,0:T(8,128)(2,1)} %shard_map.145, bf16[512,256]{1,0:T(8,128)(2,1)S(1)} %copy-done), kind=kLoop, calls=%fused_computation | loop fusion | flops 524288 | bytes 786432 | tf_op jit(solution)/shard_map/convert_element_type | solution.py:680
Async XLA Ops:
  0.0 89.1 %copy-start = (bf16[512,256]{1,0:T(8,128)(2,1)S(1)}, bf16[512,256]{1,0:T(8,128)(2,1)}, u32[]{:S(2)}) copy-start(bf16[512,256]{1,0:T(8,128)(2,1)} %args_0_.4) | copy-start | bytes 786436
